TPU v7x, 32 devices: a 4x4x1 block of a 4x4x8 slice. The times are simulated.
32 devices in a mesh: dp: 1 (over z), tp: 32 (over y, x, core).
Axes of the slice: x: 4, y: 4, z: 1, core: 2. Of those that a mesh axis runs over, the one named last changes fastest.
The devices are a block of a 4x4x8 slice.
Arguments:
- hidden: bfloat16 [4096, 512], P(('dp', 'tp'))
- targets: int32 [4096], P(('dp', 'tp'))
- loss_mask: int32 [4096], P(('dp', 'tp'))
- ln_params: float32 [2, 512], replicated
- out_embed: bfloat16 [50304, 512], P('tp')
- ln_mom1: float32 [2, 512], replicated
- ln_mom2: float32 [2, 512], replicated
- embed_mom1: float32 [50304, 512], P('tp')
- embed_mom2: float32 [50304, 512], P('tp')
Outputs:
- output 1: float32 [4096], P(('dp', 'tp'))
- output 2: float32 [1], P('dp')
- output 3: bfloat16 [4096, 512], P(('dp', 'tp'))
- output 4: float32 [2, 512], P('dp')
- output 5: float32 [2, 512], P('dp')
- output 6: float32 [2, 512], P('dp')
- output 7: bfloat16 [50304, 512], P(('dp', 'tp'))
- output 8: float32 [50304, 512], P(('dp', 'tp'))
- output 9: float32 [50304, 512], P(('dp', 'tp'))
All inputs are finite; a program needn't handle non-finite values.
Results may differ from a plain program's by a relative error of at most 0.001.
Values are sent between devices in bfloat16 or wider.
A program may use at most 768 MiB of HBM per device.

v0:
```python
import jax
import jax.numpy as jnp
from jax import lax
from jax.sharding import PartitionSpec as P

LN_EPS = 1e-5
BETA_ONE = 0.9
BETA_TWO = 0.95
ADAM_EPS = 1e-8
LEARN_RATE = 1e-3
WEIGHT_DECAY = 0.1
ADAM_STEP = 10


def layer_norm(hidden, ln_params):
    rows_f32 = hidden.astype(jnp.float32)
    row_mean = jnp.mean(rows_f32, axis=-1, keepdims=True)
    centered = rows_f32 - row_mean
    row_var = jnp.mean(centered * centered, axis=-1, keepdims=True)
    normed = centered * lax.rsqrt(row_var + LN_EPS)
    return normed * ln_params[0] + ln_params[1]


def adam_step(param_val, grad_val, m_old, v_old, decay_rate):
    m_new = BETA_ONE * m_old + (1.0 - BETA_ONE) * grad_val
    v_new = BETA_TWO * v_old + (1.0 - BETA_TWO) * grad_val * grad_val
    m_hat = m_new / (1.0 - BETA_ONE ** ADAM_STEP)
    v_hat = v_new / (1.0 - BETA_TWO ** ADAM_STEP)
    new_param = param_val - LEARN_RATE * (m_hat / (jnp.sqrt(v_hat) + ADAM_EPS) + decay_rate * param_val)
    return new_param, m_new, v_new


def solution(mesh):
    row_spec = P(("dp", "tp"), None)
    tok_spec = P(("dp", "tp"))
    vocab_spec = P("tp", None)
    repl_spec = P()
    part_spec = P("dp", None)

    def device_step(hidden, targets, loss_mask, ln_params, out_embed, ln_mom1, ln_mom2, embed_mom1, embed_mom2):
        tok_local = hidden.shape[0]
        vocab_local = out_embed.shape[0]
        shard_idx = lax.axis_index("tp")
        x_norm, ln_vjp = jax.vjp(layer_norm, hidden, ln_params)
        x_full = lax.all_gather(x_norm.astype(jnp.bfloat16), "tp", tiled=True)
        tgt_full = lax.all_gather(targets, "tp", tiled=True)
        mask_full = lax.all_gather(loss_mask, "tp", tiled=True).astype(jnp.float32)
        logits = lax.dot_general(x_full, out_embed, (((1,), (1,)), ((), ())), preferred_element_type=jnp.float32)
        local_ids = jnp.arange(vocab_local, dtype=jnp.int32) + shard_idx * vocab_local
        is_target = local_ids[None, :] == tgt_full[:, None]
        local_max = jnp.max(logits, axis=1)
        local_sum = jnp.sum(jnp.exp(logits - local_max[:, None]), axis=1)
        tgt_logit = jnp.sum(jnp.where(is_target, logits, 0.0), axis=1)
        global_max = lax.pmax(local_max, "tp")
        shard_stats = lax.psum(jnp.stack([local_sum * jnp.exp(local_max - global_max), tgt_logit]), "tp")
        log_norm = global_max + jnp.log(shard_stats[0])
        loss_full = (log_norm - shard_stats[1]) * mask_full
        valid_count = jnp.sum(mask_full)
        mean_loss = (jnp.sum(loss_full) / valid_count).reshape(1)
        token_loss = lax.dynamic_slice_in_dim(loss_full, shard_idx * tok_local, tok_local)
        tok_scale = mask_full / valid_count
        d_logits = ((jnp.exp(logits - log_norm[:, None]) - is_target.astype(jnp.float32)) * tok_scale[:, None]).astype(jnp.bfloat16)
        d_embed = lax.dot_general(d_logits, x_full, (((0,), (0,)), ((), ())), preferred_element_type=jnp.float32)
        d_x_part = jnp.dot(d_logits, out_embed, preferred_element_type=jnp.float32)
        d_x = lax.psum_scatter(d_x_part, "tp", scatter_dimension=0, tiled=True)
        d_hidden, d_ln = ln_vjp(d_x)
        d_ln = lax.psum(d_ln, "tp")
        ln_new, ln_mom1_new, ln_mom2_new = adam_step(ln_params, d_ln, ln_mom1, ln_mom2, 0.0)
        embed_f, embed_mom1_new, embed_mom2_new = adam_step(out_embed.astype(jnp.float32), d_embed, embed_mom1, embed_mom2, WEIGHT_DECAY)
        return (token_loss, mean_loss, d_hidden, ln_new, ln_mom1_new, ln_mom2_new, embed_f.astype(jnp.bfloat16), embed_mom1_new, embed_mom2_new)

    return jax.shard_map(device_step, mesh=mesh, in_specs=(row_spec, tok_spec, tok_spec, repl_spec, vocab_spec, repl_spec, repl_spec, vocab_spec, vocab_spec), out_specs=(tok_spec, P("dp"), row_spec, part_spec, part_spec, part_spec, row_spec, row_spec, row_spec), check_vma=False)
```

profile of v0, /device:TPU:97, one launch (start us, length us, event | category | flops | bytes accessed | tf_op | source)
XLA Modules:
  0.0 364.2 jit_solution(2018473709991822647)
XLA Ops:
  7.2 0.1 all-gather.4.cloned.1.call-start
  7.3 0.8 fusion.25
  8.0 1.0 convert_reduce_fusion
  9.1 1.1 fusion.17
  10.2 1.7 fusion.15
  11.8 0.1 all-gather.4.cloned.1.call-update
  11.9 0.1 reduce-scatter.2.cloned.1.call-start
  12.0 31.7 %all-gather.1 = s32[32,1,128]{2,1,0:T(1,128)S(1)} all-gather(s32[1,1,128]{2,1,0:T(1,128)} %bitcast.32), channel_id=1, replica_groups=mesh['dp'=1,'tp'=32] {'tp'}, dimensions={0}, use_global_device_ids=true | all-gather | bytes 16896 | tf_op jit(solution)/shard_map/all_gather | solution.py:47
  43.7 32.3 %all-gather = s32[32,1,128]{2,1,0:T(1,128)S(1)} all-gather(s32[1,1,128]{2,1,0:T(1,128)} %bitcast.33), channel_id=1, replica_groups=mesh['dp'=1,'tp'=32] {'tp'}, dimensions={0}, use_global_device_ids=true | all-gather | bytes 16896 | tf_op jit(solution)/shard_map/all_gather | solution.py:46
  76.0 0.6 convert_reduce_fusion.1
  76.6 14.1 %fusion.26 = (f32[4096]{0:T(1024)S(1)}, f32[4096,1572]{0,1:T(8,128)}) fusion(bf16[4096,512]{1,0:T(8,128)(2,1)} %all-gather.4.cloned.1.call-done, bf16[1572,512]{1,0:T(8,128)(2,1)} %param.13), kind=kOutput, calls=%fused_computation.50 | convolution fusion | flops 6599880704 | bytes 31576064 | tf_op jit(solution)/shard_map/dot_general | solution.py:48
  90.7 48.4 %pmax.7 = f32[4096]{0:T(1024)S(1)} all-reduce(f32[4096]{0:T(1024)S(1)} %get-tuple-element.30), channel_id=1, replica_groups=mesh['dp'=1,'tp'=32] {'tp'}, use_global_device_ids=true, to_apply=%region_3.0 | all-reduce | flops 4096 | bytes 32768 | tf_op jit(solution)/shard_map/pmax | solution.py:54
  139.1 11.8 %exponential_reduce_fusion = (f32[4096]{0:T(1024)S(1)}, f32[4096]{0:T(1024)S(1)}) fusion(f32[4096,1572]{0,1:T(8,128)} %get-tuple-element.31, f32[4096]{0:T(1024)S(1)} %get-tuple-element.30, s32[4096]{0:T(1024)S(1)} %bitcast.19, s32[1572]{0:T(1024)S(1)} %iota_add_fusion), kind=kLoop, calls=%fused_computation.6 | loop fusion | flops 32186368 | bytes 25827472 | tf_op jit(solution)/shard_map/reduce_sum | solution.py:52
  150.9 45.0 %psum.14 = f32[2,4096]{1,0:T(2,128)S(1)} all-reduce(f32[2,4096]{1,0:T(2,128)S(1)} %pad_maximum_fusion), channel_id=1, replica_groups=mesh['dp'=1,'tp'=32] {'tp'}, use_global_device_ids=true, to_apply=%region_6.7 | all-reduce | flops 8192 | bytes 65536 | tf_op jit(solution)/shard_map/psum | solution.py:55
  195.9 1.3 fusion.24
  197.2 11.9 %fusion.3 = bf16[4096,1572]{0,1:T(8,128)(2,1)S(1)} fusion(f32[4096,1572]{0,1:T(8,128)} %get-tuple-element.31, f32[4096]{0:T(1024)S(1)} %get-tuple-element.27, f32[4096]{0:T(1024)S(1)} %get-tuple-element.24, s32[4096]{0:T(1024)S(1)} %bitcast.20, s32[1572]{0:T(1024)S(1)} %iota_add_fusion), kind=kLoop, calls=%fused_computation.5 | loop fusion | flops 38633472 | bytes 38688912 | tf_op jit(solution)/shard_map/convert_element_type | solution.py:62
  209.1 0.0 copy-start
  209.1 4.6 %copy-done = bf16[4096,1572]{0,1:T(8,128)(2,1)} copy-done((bf16[4096,1572]{0,1:T(8,128)(2,1)}, bf16[4096,1572]{0,1:T(8,128)(2,1)S(1)}, u32[]{:S(2)}) %copy-start) | copy-done | bytes 12877848
  213.8 0.0 copy-done.5
  213.8 10.3 %fusion.27 = f32[4096,512]{1,0:T(8,128)} fusion(bf16[4096,1572]{0,1:T(8,128)(2,1)S(1)} %fusion.3, bf16[1572,512]{1,0:T(8,128)(2,1)S(1)} %copy-done.5), kind=kOutput, calls=%fused_computation.51 | convolution fusion | flops 6593445888 | bytes 22876160 | tf_op jit(solution)/shard_map/dot_general | solution.py:64
  224.1 0.1 reduce-scatter.2.cloned.1.call-update
  225.5 0.6 dynamic_slice.3
  226.1 16.0 %fusion.6 = (bf16[1572,512]{1,0:T(8,128)(2,1)}, f32[1572,512]{1,0:T(8,128)}, f32[1572,512]{1,0:T(8,128)}) fusion(bf16[1572,512]{1,0:T(8,128)(2,1)S(1)} %copy-done.5, f32[1572,512]{1,0:T(8,128)} %param.16, f32[1572,512]{1,0:T(8,128)} %param.17, bf16[4096,1572]{0,1:T(8,128)(2,1)} %copy-done, bf16[4096,512]{1,0:T(8,128)(2,1)} %all-gather.4.cloned.1.call-done), kind=kOutput, calls=%fused_computation.12 | convolution fusion | flops 6607128576 | bytes 33169408 | tf_op jit(solution)/shard_map/dot_general | solution.py:63
  242.1 63.9 %reduce-scatter.2.cloned.1.call-done = f32[128,512]{1,0:T(8,128)} async-done(((f32[4096,512]{1,0:T(8,128)}), f32[128,512]{1,0:T(8,128)}) %reduce-scatter.2.cloned.1.call-update) | async-done | bytes 262160 | tf_op jit(solution)/shard_map/reduce_scatter | solution.py:65
  306.0 0.0 copy-done.1
  306.0 1.2 fusion.16
  307.2 1.2 fusion.23
  308.4 46.5 %psum.15 = f32[2,512]{1,0:T(2,128)S(1)} all-reduce(f32[2,512]{1,0:T(2,128)S(1)} %pad_add_fusion), channel_id=1, replica_groups=mesh['dp'=1,'tp'=32] {'tp'}, use_global_device_ids=true, to_apply=%region_14.15 | all-reduce | flops 1024 | bytes 8192 | tf_op jit(solution)/shard_map/psum | solution.py:67
  354.9 0.7 add_convert_fusion
  355.6 0.0 copy-done.2
  355.6 0.0 copy-done.3
  355.6 0.6 multiply_subtract_fusion
  (17 shorter events, 0.1 us)
Async XLA Ops:
  7.2 69.4 %all-gather.4.cloned.1.call-start = ((), (), s32[]{:S(2)}) async-start(), calls=%async_computation.1 | async-start | bytes 4325376 | tf_op jit(solution)/shard_map/all_gather | solution.py:45
  11.9 294.1 %reduce-scatter.2.cloned.1.call-start = ((), (), s32[]{:S(2)}) async-start(), calls=%async_computation.2 | async-start | bytes 8650752 | tf_op jit(solution)/shard_map/reduce_scatter | solution.py:65
  197.2 16.6 %copy-start.5 = (bf16[1572,512]{1,0:T(8,128)(2,1)S(1)}, bf16[1572,512]{1,0:T(8,128)(2,1)}, u32[]{:S(2)}) copy-start(bf16[1572,512]{1,0:T(8,128)(2,1)} %param.13) | copy-start | bytes 4829188
  209.1 4.6 %copy-start = (bf16[4096,1572]{0,1:T(8,128)(2,1)}, bf16[4096,1572]{0,1:T(8,128)(2,1)S(1)}, u32[]{:S(2)}) copy-start(bf16[4096,1572]{0,1:T(8,128)(2,1)S(1)} %fusion.3) | copy-start | bytes 38633476
  226.1 79.9 %copy-start.1 = (bf16[128,512]{1,0:T(8,128)(2,1)S(1)}, bf16[128,512]{1,0:T(8,128)(2,1)}, u32[]{:S(2)}) copy-start(bf16[128,512]{1,0:T(8,128)(2,1)} %param.9) | copy-start | bytes 393220
  226.1 129.6 %copy-start.2 = (f32[2,512]{1,0:T(2,128)S(1)}, f32[2,512]{1,0:T(2,128)}, u32[]{:S(2)}) copy-start(f32[2,512]{1,0:T(2,128)} %param.12) | copy-start | bytes 12292
  226.1 129.6 %copy-start.3 = (f32[2,512]{1,0:T(2,128)S(1)}, f32[2,512]{1,0:T(2,128)}, u32[]{:S(2)}) copy-start(f32[2,512]{1,0:T(2,128)} %param.14) | copy-start | bytes 12292
  226.1 129.6 %copy-start.4 = (f32[2,512]{1,0:T(2,128)S(1)}, f32[2,512]{1,0:T(2,128)}, u32[]{:S(2)}) copy-start(f32[2,512]{1,0:T(2,128)} %param.15) | copy-start | bytes 12292
Sparse Core Ops, SparseCore 0:
  12.0 45.1 all-gather.3
  224.3 81.6 reduce-scatter.1
where the time goes:
time: 365 us; the launch traced here: 364 us
  blocking collectives  204 us (56%)
  waiting for transfers between devices  64 us (18%)
  matrix products  40.4 us (11%)
  other arithmetic  33.2 us (9%)
  between operations  16.7 us (5%)
  local copies, waits for them, and re-layouts  6.02 us (2%)
    reduce_scatter x1, waiting for transfers between devices, device_step(): d_x = lax.psum_scatter(d_x_part, 'tp', scatter_dimension=0, tiled=True)  63.9 us
    pmax x1, blocking collectives, device_step(): global_max = lax.pmax(local_max, 'tp')  48.4 us
    psum x1, blocking collectives, device_step(): d_ln = lax.psum(d_ln, 'tp')  46.5 us
    psum x1, blocking collectives, device_step(): lax.psum(jnp.stack([local_sum * jnp.exp(local_max - global_max), tgt_logi...  45 us
    all_gather x1, blocking collectives, device_step(): tgt_full = lax.all_gather(targets, 'tp', tiled=True)  32.3 us
    all_gather x1, blocking collectives, device_step(): mask_full = lax.all_gather(loss_mask, 'tp', tiled=True).astype(jnp.float32)  31.7 us
    dot_general x1, matrix products, device_step(): lax.dot_general(d_logits, x_full, (((0,), (0,)), ((), ())), preferred_ele...  16 us
    dot_general x1, matrix products, device_step(): lax.dot_general(x_full, out_embed, (((1,), (1,)), ((), ())), preferred_el...  14.1 us
  transfers between devices with their start and end apart: 2, of which 1 were waited for; matrix products, arithmetic and copies ran while one was open for 5% of the time, Pallas kernels for 0%

commit v1 on v0

v1 whole, which is shorter than its diff:
```python
import functools
import math

import jax
import jax.numpy as jnp
from jax import lax
from jax.experimental import pallas as pl
from jax.experimental.pallas import tpu as pltpu
from jax.sharding import PartitionSpec as P

LN_EPS = 1e-5
BETA_ONE = 0.9
BETA_TWO = 0.95
ADAM_EPS = 1e-8
LEARN_RATE = 1e-3
WEIGHT_DECAY = 0.1
ADAM_STEP = 10
MESH = pl.DeviceIdType.MESH
CORES = 2
PAIR = (0, 1)
LAST = (2, 3)
ANY = pl.BlockSpec(memory_space=pl.ANY)
VMEM = pl.BlockSpec(memory_space=pltpu.VMEM)
F32, BF16 = jnp.float32, jnp.bfloat16
NN = (((1,), (0,)), ((), ()))
NT = (((1,), (1,)), ((), ()))


def adam_step(param_val, grad_val, m_old, v_old, decay_rate):
    m_new = BETA_ONE * m_old + (1.0 - BETA_ONE) * grad_val
    v_new = BETA_TWO * v_old + (1.0 - BETA_TWO) * grad_val * grad_val
    m_hat = m_new / (1.0 - BETA_ONE ** ADAM_STEP)
    v_hat = v_new / (1.0 - BETA_TWO ** ADAM_STEP)
    new_param = param_val - LEARN_RATE * (m_hat / (jnp.sqrt(v_hat) + ADAM_EPS) + decay_rate * param_val)
    return new_param, m_new, v_new


def row_tiles(rows, size):
    return [(r, min(size, rows - r)) for r in range(0, rows, size)]


def step_kernel(side, hid_ref, tgt_ref, msk_ref, lnp_ref, emb_ref,
                dE_out, dh_out, dln_out, loss_out, mean_out,
                xg, ee, et, ez, dz, dxp, r1, r2, t2, q1, q2,
                tm_all, st_all, tgt_ck, msk_ck, rel_ck, a_ck, s_ck, loss_ck, pair, dl_all, fin,
                loc_sem, ag_s, ag_r, tm_s, tm_r, st_s, st_r, rs_s, rs_r, dl_s, dl_r, pr_s, pr_r, free_sem):
    chips = side * side
    ndev = chips * CORES
    tok = hid_ref.shape[0]
    half = tok // 2
    dim = hid_ref.shape[1]
    voc = emb_ref.shape[0]
    ct = half * side
    nck = 2 * side
    hd = dim // 2
    me = lax.axis_index("tp")
    core = lax.rem(me, CORES)
    chip = me // CORES
    mx, my = lax.rem(chip, side), chip // side
    sib = me + 1 - 2 * core

    def dev(y, x):
        return {"tp": (lax.rem(y, side) * side + lax.rem(x, side)) * CORES + core}

    def dev_minor(g, d):
        return dev(my, mx + d) if g == 0 else dev(my + d, mx)

    def dev_major(g, d):
        return dev(my + d, mx) if g == 0 else dev(my, mx + d)

    maj = (my, mx)
    mnr = (mx, my)

    def chunk_of(g, d):
        return g * side + lax.rem(maj[g] + d, side)

    def rcopy(src, dst, ssem, rsem, device):
        return pltpu.make_async_remote_copy(src_ref=src, dst_ref=dst, send_sem=ssem, recv_sem=rsem,
                                            device_id=device, device_id_type=MESH)

    e_local = pltpu.make_async_copy(emb_ref, ee.at[0], loc_sem.at[0])
    e_local.start()
    barrier = pltpu.get_barrier_semaphore()
    for d in range(1, ndev):
        pl.semaphore_signal(barrier, inc=1, device_id={"tp": lax.rem(me + d, ndev)}, device_id_type=MESH)

    rows = hid_ref[...].astype(F32)
    cent = rows - jnp.mean(rows, axis=-1, keepdims=True)
    rstd = lax.rsqrt(jnp.mean(cent * cent, axis=-1, keepdims=True) + LN_EPS)
    xb = (cent * rstd * lnp_ref[0:1, :] + lnp_ref[1:2, :]).astype(BF16)

    def xslot(c, pos, r0=0, n=half):
        return xg.at[pl.ds(pl.multiple_of(c * ct + pos * half + r0, 32), n)]

    for g in PAIR:
        xslot_rows = pl.ds(pl.multiple_of(chunk_of(g, 0) * ct + mnr[g] * half, half), half)
        xg[xslot_rows, :] = xb[g * half:(g + 1) * half]
    tm_all[chip, 0:1, :] = tgt_ref[...]
    tm_all[chip, 1:2, :] = msk_ref[...]
    tm_all[chip, 2:8, :] = jnp.zeros((6, tok), jnp.int32)
    et[:, :, voc:] = jnp.zeros((2, dim, et.shape[2] - voc), BF16)

    pl.semaphore_wait(barrier, ndev - 1)

    def ag1(g, k):
        c, p = chunk_of(g, 0), mnr[g]
        if k < 2:
            s = xslot(c, p)
            return rcopy(s, s, ag_s.at[g, 0, k], ag_r.at[g, 0, k], dev_minor(g, (1, side - 1)[k]))
        q = lax.rem(p + (side - 1, 1)[k - 2], side)
        s = xslot(c, q, (0, half // 2)[k - 2], half // 2)
        return rcopy(s, s, ag_s.at[g, 0, k], ag_r.at[g, 0, k], dev_minor(g, (1, side - 1)[k - 2]))

    def ag1_recv(g, k):
        c, p = chunk_of(g, 0), mnr[g]
        if k < 2:
            s = xslot(c, lax.rem(p + (side - 1, 1)[k], side))
        else:
            s = xslot(c, lax.rem(p + 2, side), (0, half // 2)[k - 2], half // 2)
        rcopy(s, s, ag_s.at[g, 0, k], ag_r.at[g, 0, k], dev_minor(g, 1)).wait_recv()

    def cslot(c, r0, n):
        return xg.at[pl.ds(pl.multiple_of(c * ct + r0, 32), n)]

    def ag2(g, k):
        if k < 2:
            s = cslot(chunk_of(g, 0), 0, ct)
            return rcopy(s, s, ag_s.at[g, 1, k], ag_r.at[g, 1, k], dev_major(g, (1, side - 1)[k]))
        s = cslot(chunk_of(g, (side - 1, 1)[k - 2]), (0, ct // 2)[k - 2], ct // 2)
        return rcopy(s, s, ag_s.at[g, 1, k], ag_r.at[g, 1, k], dev_major(g, (1, side - 1)[k - 2]))

    def ag2_recv(g, k):
        if k < 2:
            s = cslot(chunk_of(g, (side - 1, 1)[k]), 0, ct)
        else:
            s = cslot(chunk_of(g, 2), (0, ct // 2)[k - 2], ct // 2)
        rcopy(s, s, ag_s.at[g, 1, k], ag_r.at[g, 1, k], dev_major(g, 1)).wait_recv()

    for k in PAIR:
        for g in PAIR:
            ag1(g, k).start()
    e_send = rcopy(emb_ref, ee.at[1], pr_s.at[0], pr_r.at[0], {"tp": sib})
    e_send.start()
    tms = []
    for d in range(1, chips):
        t = lax.rem(chip + d, chips)
        cp = rcopy(tm_all.at[chip], tm_all.at[chip], tm_s.at[d], tm_r.at[d], {"tp": t * CORES + core})
        cp.start()
        tms.append(cp)

    for k in PAIR:
        for g in PAIR:
            ag1_recv(g, k)
            ag1(g, k + 2).start()

    def transpose_e(h):
        for r0, n in row_tiles(voc, 384):
            et[h, :, r0:r0 + n] = ee[h, r0:r0 + n, :].T

    e_local.wait()
    transpose_e(0)

    for k in LAST:
        for g in PAIR:
            ag1_recv(g, k)
    for k in PAIR:
        for g in PAIR:
            ag2(g, k).start()

    for d in range(1, chips):
        s = tm_all.at[lax.rem(chip + chips - d, chips)]
        rcopy(s, s, tm_s.at[d], tm_r.at[d], {"tp": me}).wait_recv()
    lane = lax.broadcasted_iota(jnp.int32, (8, tok), 1)
    for c in range(nck):
        for j in range(ct // tok):
            if c < side:
                a, b = tm_all[c * side + 2 * j], tm_all[c * side + 2 * j + 1]
                v = jnp.where(lane < half, a, pltpu.roll(b, half, 1))
            else:
                a, b = tm_all[2 * j * side + c - side], tm_all[(2 * j + 1) * side + c - side]
                v = jnp.where(lane < half, pltpu.roll(a, half, 1), b)
            tgt_ck[c:c + 1, j * tok:(j + 1) * tok] = v[0:1]
            msk_ck[c:c + 1, j * tok:(j + 1) * tok] = v[1:2]
    own = tgt_ck[...] - me * voc
    oth = tgt_ck[...] - sib * voc
    rel_ck[0] = own
    rel_ck[1] = oth
    maskf = msk_ck[...].astype(F32)
    cnt = jnp.sum(maskf, keepdims=True)
    pair[0] = jnp.broadcast_to(cnt, (8, tok))
    cnt_send = rcopy(pair.at[0], pair.at[1], pr_s.at[1], pr_r.at[1], {"tp": sib})
    cnt_send.start()

    e_send.wait_recv()
    transpose_e(1)

    def logits_chunk(c):
        x_c = xg[pl.ds(pl.multiple_of(c * ct, ct), ct), :]
        pair_i, lane0 = c // 2, pl.multiple_of(lax.rem(c, 2) * ct, ct)
        top = None
        for h in PAIR:
            for r0, n in row_tiles(voc, 528):
                z = lax.dot_general(ee[h, r0:r0 + n, :], x_c, NT, preferred_element_type=F32)
                ez[pair_i, h, r0:r0 + n, pl.ds(lane0, ct)] = z
                t = jnp.max(z, axis=0, keepdims=True)
                top = t if top is None else jnp.maximum(top, t)
        tot = jnp.zeros((1, ct), F32)
        tl = jnp.zeros((1, ct), F32)
        for h in PAIR:
            rel = rel_ck[h, pl.ds(c, 1), :]
            for r0, n in row_tiles(voc, 528):
                z = ez[pair_i, h, r0:r0 + n, pl.ds(lane0, ct)]
                e = jnp.exp(z - top)
                ez[pair_i, h, r0:r0 + n, pl.ds(lane0, ct)] = e
                tot += jnp.sum(e, axis=0, keepdims=True)
                hit = lax.broadcasted_iota(jnp.int32, (n, ct), 0) == rel - r0
                tl += jnp.sum(jnp.where(hit, z, 0.0), axis=0, keepdims=True)
        st_all[chip, 0, pl.ds(c, 1), :] = top
        st_all[chip, 1, pl.ds(c, 1), :] = tot
        st_all[chip, 2, pl.ds(c, 1), :] = tl

    def both(fn, d):
        def body(g, carry):
            m = my + g * (mx - my)
            fn(g * side + lax.rem(m + d, side))
            return carry
        lax.fori_loop(0, 2, body, 0)

    both(logits_chunk, 0)
    for k in PAIR:
        for g in PAIR:
            ag2_recv(g, k)
            ag2(g, k + 2).start()
    both(logits_chunk, 1)
    both(logits_chunk, side - 1)
    for k in LAST:
        for g in PAIR:
            ag2_recv(g, k)
    both(logits_chunk, 2)

    sts = []
    for d in range(1, chips):
        t = lax.rem(chip + d, chips)
        cp = rcopy(st_all.at[chip], st_all.at[chip], st_s.at[d], st_r.at[d], {"tp": t * CORES + core})
        cp.start()
        sts.append(cp)
    rcopy(pair.at[0], pair.at[1], pr_s.at[1], pr_r.at[1], {"tp": sib}).wait_recv()
    total_n = (pair[0] + pair[1])[0:1, 0:1]
    scale = maskf / total_n
    s_ck[...] = scale
    for d in range(1, chips):
        s = st_all.at[lax.rem(chip + chips - d, chips)]
        rcopy(s, s, st_s.at[d], st_r.at[d], {"tp": me}).wait_recv()
    gmax = st_all[0, 0]
    for t in range(1, chips):
        gmax = jnp.maximum(gmax, st_all[t, 0])
    gsum = jnp.zeros_like(gmax)
    gtl = jnp.zeros_like(gmax)
    for t in range(chips):
        gsum += st_all[t, 1] * jnp.exp(st_all[t, 0] - gmax)
        gtl += st_all[t, 2]
    lse = gmax + jnp.log(gsum)
    a_ck[...] = jnp.exp(st_all[chip, 0] - lse) * scale
    loss = (lse - gtl) * maskf
    loss_ck[...] = loss
    lsum = jnp.sum(loss, keepdims=True)
    pair[2] = jnp.broadcast_to(lsum, (8, tok))
    loss_send = rcopy(pair.at[2], pair.at[3], pr_s.at[2], pr_r.at[2], {"tp": sib})
    loss_send.start()

    def grad_chunk(c):
        pair_i, lane0 = c // 2, pl.multiple_of(lax.rem(c, 2) * ct, ct)
        out0 = pl.multiple_of(c * ct, ct)
        a = a_ck[pl.ds(c, 1), :]
        s = s_ck[pl.ds(c, 1), :]
        acc = None
        for h in PAIR:
            rel = rel_ck[h, pl.ds(c, 1), :]
            for r0, n in row_tiles(voc, 528):
                e = ez[pair_i, h, r0:r0 + n, pl.ds(lane0, ct)]
                hit = lax.broadcasted_iota(jnp.int32, (n, ct), 0) == rel - r0
                dz[h, r0:r0 + n, pl.ds(out0, ct)] = (e * a - jnp.where(hit, s, 0.0)).astype(BF16)
        for q in range(2):
            acc = None
            for h in PAIR:
                t = lax.dot_general(et[h, q * hd:(q + 1) * hd, :], dz[h, :, pl.ds(out0, ct)], NN,
                                    preferred_element_type=F32)
                acc = t if acc is None else acc + t
            dxp[c, q * hd:(q + 1) * hd, :] = acc

    dz[:, voc:, :] = jnp.zeros((2, dz.shape[1] - voc, dz.shape[2]), BF16)

    class Ring:
        def __init__(self, stage, g, piece, relay, land, device):
            self.piece, self.relay, self.land, self.device = piece, relay, land, device
            self.ss, self.rr = rs_s.at[stage, g], rs_r.at[stage, g]
        def copy(self, k):
            minus, plus = side - 1, 1
            src, dst, to = {
                0: (lambda: self.piece(2, 0), lambda: self.relay(0), minus),
                1: (lambda: self.piece(2, 1), lambda: self.relay(1), plus),
                2: (lambda: self.piece(1, 0), lambda: self.land(1), plus),
                3: (lambda: self.piece(minus, 1), lambda: self.land(2), minus),
                4: (lambda: self.piece(minus, 0), lambda: self.land(0), minus),
                5: (lambda: self.piece(1, 1), lambda: self.land(3), plus),
            }[k]
            return rcopy(src(), dst(), self.ss.at[k], self.rr.at[k], self.device(to))

    def piece1(g):
        return lambda d, q: dxp.at[chunk_of(g, d), pl.ds(q * hd, hd)]

    def piece2(g):
        return lambda d, q: t2.at[g, pl.ds(pl.multiple_of(lax.rem(mnr[g] + d, side) * half + q * (half // 2), 32), half // 2)]

    ring1 = [Ring(0, g, piece1(g), lambda i, g=g: r1.at[g, i], lambda i, g=g: r2.at[g, i],
                  functools.partial(dev_major, g)) for g in PAIR]
    ring2 = [Ring(1, g, piece2(g), lambda i, g=g: q1.at[g, i], lambda i, g=g: q2.at[g, i],
                  functools.partial(dev_minor, g)) for g in PAIR]

    both(grad_chunk, 2)
    for k in PAIR:
        for g in PAIR:
            ring1[g].copy(k).start()
    both(grad_chunk, 1)
    for g in PAIR:
        ring1[g].copy(2).start()
    both(grad_chunk, side - 1)
    for g in PAIR:
        ring1[g].copy(3).start()
    for g in PAIR:
        ring1[g].copy(0).wait_recv()
        c = chunk_of(g, side - 1)
        dxp[c, 0:hd, :] = dxp[c, 0:hd, :] + r1[g, 0]
        ring1[g].copy(4).start()
        ring1[g].copy(1).wait_recv()
        c = chunk_of(g, 1)
        dxp[c, hd:, :] = dxp[c, hd:, :] + r1[g, 1]
        ring1[g].copy(5).start()
    both(grad_chunk, 0)
    pl.semaphore_signal(free_sem, inc=1, device_id={"tp": sib}, device_id_type=MESH)

    def embed_grad(h, dst):
        for r0, n in row_tiles(voc, 528):
            ez[0, dst, r0:r0 + n, :] = lax.dot_general(dz[h, r0:r0 + n, :], xg[...], NN, preferred_element_type=F32)

    embed_grad(1, 0)
    pl.semaphore_wait(free_sem, 1)
    de_send = rcopy(ez.at[0, 0], ez.at[1, 0], pr_s.at[3], pr_r.at[3], {"tp": sib})
    de_send.start()

    for g in PAIR:
        for k in range(2, 6):
            ring1[g].copy(k).wait_recv()
        c = chunk_of(g, 0)
        lo = dxp[c, 0:hd, :] + r2[g, 0] + r2[g, 1]
        hi = dxp[c, hd:, :] + r2[g, 2] + r2[g, 3]
        t2[g, :, 0:hd] = lo.T
        t2[g, :, hd:] = hi.T
        for k in range(4):
            ring2[g].copy(k).start()

    embed_grad(0, 1)
    de_send.wait_recv()
    for r0, n in row_tiles(voc, 528):
        ez[0, 1, r0:r0 + n, :] = ez[0, 1, r0:r0 + n, :] + ez[1, 0, r0:r0 + n, :]
    de_out = pltpu.make_async_copy(ez.at[0, 1], dE_out, loc_sem.at[1])
    de_out.start()

    hq = half // 2
    for g in PAIR:
        for k, d, q, to in ((0, side - 1, 0, 4), (1, 1, 1, 5)):
            ring2[g].copy(k).wait_recv()
            rs = pl.ds(pl.multiple_of(lax.rem(mnr[g] + d, side) * half + q * hq, 32), hq)
            t2[g, rs, :] = t2[g, rs, :] + q1[g, k]
            ring2[g].copy(to).start()
    for g in PAIR:
        for k in range(2, 6):
            ring2[g].copy(k).wait_recv()
        base = pl.multiple_of(mnr[g] * half, half)
        fin[g * half:g * half + hq, :] = t2[g, pl.ds(base, hq), :] + q2[g, 0] + q2[g, 1]
        fin[g * half + hq:(g + 1) * half, :] = t2[g, pl.ds(base + hq, hq), :] + q2[g, 2] + q2[g, 3]

    dx = fin[...]
    rows = hid_ref[...].astype(F32)
    cent = rows - jnp.mean(rows, axis=-1, keepdims=True)
    rstd = lax.rsqrt(jnp.mean(cent * cent, axis=-1, keepdims=True) + LN_EPS)
    normed = cent * rstd
    dgam = jnp.sum(dx * normed, axis=0, keepdims=True)
    dbet = jnp.sum(dx, axis=0, keepdims=True)
    for j in range(dim // tok):
        dl_all[me, j:j + 1, :] = dgam[:, j * tok:(j + 1) * tok]
        dl_all[me, 4 + j:5 + j, :] = dbet[:, j * tok:(j + 1) * tok]
    dls = []
    for d in range(1, ndev):
        cp = rcopy(dl_all.at[me], dl_all.at[me], dl_s.at[d], dl_r.at[d], {"tp": lax.rem(me + d, ndev)})
        cp.start()
        dls.append(cp)
    dn = dx * lnp_ref[0:1, :]
    dh = rstd * (dn - jnp.mean(dn, axis=-1, keepdims=True) - normed * jnp.mean(dn * normed, axis=-1, keepdims=True))
    dh_out[...] = dh.astype(BF16)

    lane1 = lax.broadcasted_iota(jnp.int32, (1, tok), 1)

    def pick(g):
        row = loss_ck[pl.ds(chunk_of(g, 0), 1), :]
        return pltpu.roll(row, lax.rem(2 * ct - mnr[g] * half + g * half, ct), 1)[:, 0:tok]

    loss_out[...] = jnp.where(lane1 < half, pick(0), pick(1))
    loss_send.wait()
    mean_out[...] = (pair[2] + pair[3])[0:1, 0:1] / total_n

    for d in range(1, ndev):
        s = dl_all.at[lax.rem(me + ndev - d, ndev)]
        rcopy(s, s, dl_s.at[d], dl_r.at[d], {"tp": me}).wait_recv()
    dl = jnp.sum(dl_all[...], axis=0)
    for j in range(dim // tok):
        dln_out[0:1, j * tok:(j + 1) * tok] = dl[j:j + 1]
        dln_out[1:2, j * tok:(j + 1) * tok] = dl[4 + j:5 + j]

    for g in PAIR:
        for k in range(4):
            ag1(g, k).wait_send()
            ag2(g, k).wait_send()
        for k in range(6):
            ring1[g].copy(k).wait_send()
            ring2[g].copy(k).wait_send()
    for cp in tms + sts + dls:
        cp.wait_send()
    e_send.wait_send()
    cnt_send.wait_send()
    de_send.wait_send()
    de_out.wait()


def adam_kernel(dE, emb, m1, m2, dln, lnp, lm1, lm2, loss, mean, dh,
                e_new, m1_new, m2_new, ln_new, lm1_new, lm2_new, loss_o, mean_o, dh_o):
    p, a, b = adam_step(emb[...].astype(F32), dE[...], m1[...], m2[...], WEIGHT_DECAY)
    e_new[...] = p.astype(BF16)
    m1_new[...] = a
    m2_new[...] = b

    @pl.when(pl.program_id(0) == 0)
    def _():
        p, a, b = adam_step(lnp[...], dln[...], lm1[...], lm2[...], 0.0)
        ln_new[...] = p
        lm1_new[...] = a
        lm2_new[...] = b
        loss_o[...] = loss[...]
        mean_o[...] = mean[...]
        dh_o[...] = dh[...]


def solution(mesh):
    ntp = mesh.shape["tp"]
    side = math.isqrt(ntp // CORES)
    row_spec = P(("dp", "tp"), None)
    tok_spec = P(("dp", "tp"))
    vocab_spec = P("tp", None)
    repl_spec = P()
    part_spec = P("dp", None)

    def device_step(hidden, targets, loss_mask, ln_params, out_embed, ln_mom1, ln_mom2, embed_mom1, embed_mom2):
        tok, dim = hidden.shape
        voc = out_embed.shape[0]
        half, chips = tok // 2, side * side
        ct, nck = half * side, 2 * side
        ntok = ct * nck
        vpad = -(-voc // 128) * 128
        dma, vm = pltpu.SemaphoreType.DMA, pltpu.VMEM
        dE, dh, dln, loss, mean = pl.pallas_call(
            functools.partial(step_kernel, side),
            out_shape=[jax.ShapeDtypeStruct((voc, dim), F32), jax.ShapeDtypeStruct((tok, dim), BF16),
                       jax.ShapeDtypeStruct((2, dim), F32), jax.ShapeDtypeStruct((1, tok), F32),
                       jax.ShapeDtypeStruct((1, 1), F32)],
            in_specs=[VMEM, VMEM, VMEM, VMEM, ANY],
            out_specs=[ANY, VMEM, VMEM, VMEM, VMEM],
            scratch_shapes=[
                vm((ntok, dim), BF16),
                vm((2, voc, dim), BF16),
                vm((2, dim, vpad), BF16),
                vm((nck // 2, 2, voc, 2 * ct), F32),
                vm((2, vpad, ntok), BF16),
                vm((nck, dim, ct), F32),
                vm((2, 2, dim // 2, ct), F32),
                vm((2, 4, dim // 2, ct), F32),
                vm((2, ct, dim), F32),
                vm((2, 2, half // 2, dim), F32),
                vm((2, 4, half // 2, dim), F32),
                vm((chips, 8, tok), jnp.int32),
                vm((chips, 3, nck, ct), F32),
                *[vm((nck, ct), jnp.int32)] * 2, vm((2, nck, ct), jnp.int32),
                *[vm((nck, ct), F32)] * 3,
                vm((4, 8, tok), F32),
                vm((ntp, 8, tok), F32),
                vm((tok, dim), F32),
                dma((2,)), *[dma((2, 2, 4))] * 2, dma((chips,)), dma((chips,)), dma((chips,)), dma((chips,)),
                *[dma((2, 2, 6))] * 2, dma((ntp,)), dma((ntp,)), *[dma((4,))] * 2,
                pltpu.SemaphoreType.REGULAR,
            ],
            compiler_params=pltpu.CompilerParams(collective_id=0, has_side_effects=True, vmem_limit_bytes=67043328),
            name="head_step",
        )(hidden, targets.reshape(1, tok), loss_mask.reshape(1, tok), ln_params, out_embed)

        blk = 264
        big = pl.BlockSpec((blk, dim), lambda i: (i, 0))

        def whole(s):
            return pl.BlockSpec(s, lambda i: (0, 0))

        small = [whole((2, dim))] * 3
        rest = [whole((1, tok)), whole((1, 1)), whole((tok, dim))]
        e_new, m1n, m2n, lnn, lm1n, lm2n, loss, mean, dh = pl.pallas_call(
            adam_kernel,
            grid=(pl.cdiv(voc, blk),),
            out_shape=[jax.ShapeDtypeStruct((voc, dim), BF16)] + [jax.ShapeDtypeStruct((voc, dim), F32)] * 2
            + [jax.ShapeDtypeStruct((2, dim), F32)] * 3
            + [jax.ShapeDtypeStruct((1, tok), F32), jax.ShapeDtypeStruct((1, 1), F32), jax.ShapeDtypeStruct((tok, dim), BF16)],
            in_specs=[big] * 4 + [whole((2, dim))] + small + rest,
            out_specs=[big] * 3 + small + rest,
            compiler_params=pltpu.CompilerParams(dimension_semantics=("arbitrary",)),
            name="adam_step",
        )(dE, out_embed, embed_mom1, embed_mom2, dln, ln_params, ln_mom1, ln_mom2, loss, mean, dh)
        return (loss.reshape(tok), mean.reshape(1), dh, lnn, lm1n, lm2n, e_new, m1n, m2n)

    return jax.shard_map(device_step, mesh=mesh, in_specs=(row_spec, tok_spec, tok_spec, repl_spec, vocab_spec, repl_spec, repl_spec, vocab_spec, vocab_spec), out_specs=(tok_spec, P("dp"), row_spec, part_spec, part_spec, part_spec, row_spec, row_spec, row_spec), check_vma=False)
```

time: 365 us -> 88.2 us (0.24)
  blocking collectives: 204 us -> 0 us
  Pallas kernels: 0 us -> 87.2 us
  waiting for transfers between devices: 64 us -> 0 us
  matrix products: 40.4 us -> 0 us
  other arithmetic: 33.2 us -> 0 us
  between operations: 16.7 us -> 0.83 us
  local copies, waits for them, and re-layouts: 6.02 us -> 0 us
    psum x2 -> x0, blocking collectives: 91.5 us -> none  [the longest x1 46.5 us: device_step(): d_ln = lax.psum(d_ln, 'tp')]
    pallas_call x0 -> x2, Pallas kernels: none -> 87.2 us  [the longest x1 76.5 us: device_step(): pl.pallas_call(functools.partial(step_kernel, side), out_shape=[jax.Shape...]
    all_gather x2 -> x0, blocking collectives: 64 us -> none  [the longest x1 32.3 us: device_step(): tgt_full = lax.all_gather(targets, 'tp', tiled=True)]
    reduce_scatter x1 -> x0, waiting for transfers between devices: 63.9 us -> none  [device_step(): d_x = lax.psum_scatter(d_x_part, 'tp', scatter_dimension=0, tiled=True)]
    pmax x1 -> x0, blocking collectives: 48.4 us -> none  [device_step(): global_max = lax.pmax(local_max, 'tp')]
    dot_general x3 -> x0, matrix products: 40.4 us -> none  [the longest x1 16 us: device_step(): lax.dot_general(d_logits, x_full, (((0,), (0,)), ((), ())), preferred_ele...]
    reduce_sum x7 -> x0, other arithmetic: 18.1 us -> none  [the longest x1 11.8 us: device_step(): local_sum = jnp.sum(jnp.exp(logits - local_max[:, None]), axis=1)]
    convert_element_type x4 -> x0, other arithmetic: 14.4 us -> none  [the longest x1 11.9 us: device_step(): ((jnp.exp(logits - log_norm[:, None]) - is_target.astype(jnp.float32)) *...]
  transfers between devices with their start and end apart: 2 -> 0, of which waited for: 1 -> 0; matrix products, arithmetic and copies ran while one was open for 5% -> 0% of each run, Pallas kernels for 0% -> 0%
where the time goes in v1:
time: 88.2 us; the launch traced here: 88 us
  Pallas kernels  87.2 us (99%)
    pallas_call x1, Pallas kernels, device_step(): pl.pallas_call(functools.partial(step_kernel, side), out_shape=[jax.Shape...  76.5 us
    pallas_call x1, Pallas kernels, device_step(): pl.pallas_call(adam_kernel, grid=(pl.cdiv(voc, blk),), out_shape=[jax.Sha...  10.7 us

profile of v1, /device:TPU:97, one launch (start us, length us, event | category | flops | bytes accessed | tf_op | source)
XLA Modules:
  0.0 88.0 jit_solution(9802700060079668992)
XLA Ops:
  0.6 76.5 %head_step.1 = (f32[1572,512]{1,0:T(8,128)}, bf16[128,512]{1,0:T(8,128)(2,1)}, f32[2,512]{1,0:T(2,128)}, f32[1,128]{1,0:T(1,128)}, f32[1,1]{1,0:T(1,128)}) custom-call(bf16[128,512]{1,0:T(8,128)(2,1)} %hid_ref.1, s32[1,128]{1,0:T(1,128)} %bitcast.4, s32[1,128]{1,0:T(1,128)} %bitcast.5, f32[2,512]{1,0:T(2,128)} %lnp.1, bf16[1572,512]{1,0:T(8,128)(2,1)} %emb.1), custom_call_target="tpu_custom_call" | custom-call | tf_op jit(solution)/shard_map/head_step/pallas_call | solution.py:470
  77.1 10.7 %adam_step.1 = (bf16[1572,512]{1,0:T(8,128)(2,1)}, f32[1572,512]{1,0:T(8,128)}, f32[1572,512]{1,0:T(8,128)}, f32[2,512]{1,0:T(2,128)}, f32[2,512]{1,0:T(2,128)},...) custom-call(f32[1572,512]{1,0:T(8,128)} %get-tuple-element.23.dE, ...), custom_call_target="tpu_custom_call" | custom-call | tf_op jit(solution)/shard_map/adam_step/pallas_call | solution.py:512

commit v2 on v0

v2 whole, which is shorter than its diff:
```python
import functools
import math

import jax
import jax.numpy as jnp
from jax import lax
from jax.experimental import pallas as pl
from jax.experimental.pallas import tpu as pltpu
from jax.sharding import PartitionSpec as P

LN_EPS = 1e-5
BETA_ONE = 0.9
BETA_TWO = 0.95
ADAM_EPS = 1e-8
LEARN_RATE = 1e-3
WEIGHT_DECAY = 0.1
ADAM_STEP = 10
MESH = pl.DeviceIdType.MESH
CORES = 2
PAIR = (0, 1)
TILE = 528
ANY = pl.BlockSpec(memory_space=pl.ANY)
F32, BF16 = jnp.float32, jnp.bfloat16
NN = (((1,), (0,)), ((), ()))
NT = (((1,), (1,)), ((), ()))


def adam_step(param_val, grad_val, m_old, v_old, decay_rate):
    m_new = BETA_ONE * m_old + (1.0 - BETA_ONE) * grad_val
    v_new = BETA_TWO * v_old + (1.0 - BETA_TWO) * grad_val * grad_val
    m_hat = m_new / (1.0 - BETA_ONE ** ADAM_STEP)
    v_hat = v_new / (1.0 - BETA_TWO ** ADAM_STEP)
    new_param = param_val - LEARN_RATE * (m_hat / (jnp.sqrt(v_hat) + ADAM_EPS) + decay_rate * param_val)
    return new_param, m_new, v_new


def row_tiles(rows, size):
    return [(r, min(size, rows - r)) for r in range(0, rows, size)]


def step_kernel(side, hid_hbm, tgt_hbm, msk_hbm, lnp_hbm, emb_ref,
                dE_out, dh_out, dln_out, sm_out,
                hid_ref, tgt_ref, msk_ref, lnp_ref, dh_buf, dln_buf, sm_buf,
                xg, ee, et, ez, dz, dxp, r1, r2, q1, q2,
                tm_all, st_all, tl_all, tgt_ck, msk_ck, rel_ck, top_ck, lse_ck, s_ck, loss_ck, pair, dl_all,
                in_sem, out_sem, ag1_s, ag1_r, ag2_s, ag2_r, ag3_s, ag3_r, tm_s, tm_r, st_s, st_r, tl_s, tl_r,
                rs_s, rs_r, ring_s, ring_r, dl_s, dl_r, pr_s, pr_r, free_sem):
    chips = side * side
    ndev = chips * CORES
    tok, dim = hid_ref.shape
    half = tok // 2
    voc = emb_ref.shape[0]
    pairs = side // 2
    ct = 2 * tok
    nck = side * pairs
    hd, qd = dim // 2, dim // 4
    plus, minus = 1, side - 1
    me = lax.axis_index("tp")
    core = lax.rem(me, CORES)
    chip = me // CORES
    mx, my = lax.rem(chip, side), chip // side
    odd = lax.rem(mx, 2)
    sib = me + 1 - 2 * core

    def chip_at(dy, dx):
        return lax.rem(my + dy, side) * side + lax.rem(mx + dx, side)

    def rel(g, dmaj, dmin):
        return (dmin, dmaj) if g else (dmaj, dmin)

    def dev(g, dmaj, dmin):
        return {"tp": chip_at(*rel(g, dmaj, dmin)) * CORES + core}

    def rcopy(src, dst, ssem, rsem, device):
        return pltpu.make_async_remote_copy(src_ref=src, dst_ref=dst, send_sem=ssem, recv_sem=rsem,
                                            device_id=device, device_id_type=MESH)

    loads = [pltpu.make_async_copy(s, d, in_sem.at[i]) for i, (s, d) in enumerate(
        ((hid_hbm, hid_ref), (lnp_hbm, lnp_ref), (tgt_hbm, tgt_ref), (msk_hbm, msk_ref), (emb_ref, ee.at[0])))]
    for cp in loads:
        cp.start()
    barrier = pltpu.get_barrier_semaphore()
    for d in range(1, ndev):
        pl.semaphore_signal(barrier, inc=1, device_id={"tp": lax.rem(me + d, ndev)}, device_id_type=MESH)
    for cp in loads[:4]:
        cp.wait()

    def normalize():
        rows = hid_ref[...].astype(F32)
        cent = rows - jnp.mean(rows, axis=-1, keepdims=True)
        rstd = lax.rsqrt(jnp.mean(cent * cent, axis=-1, keepdims=True) + LN_EPS)
        return cent * rstd, rstd

    xb = (normalize()[0] * lnp_ref[0:1, :] + lnp_ref[1:2, :]).astype(BF16)

    def xslot(g, dmaj, dmin, r0=0, n=half):
        row = chip_at(*rel(g, dmaj, dmin)) * tok + g * half + r0
        return xg.at[pl.ds(pl.multiple_of(row, 32), n)]

    xg[pl.ds(pl.multiple_of(chip * tok, tok), tok), :] = xb
    tm_all[chip, 0:1, :] = tgt_ref[...]
    tm_all[chip, 1:2, :] = msk_ref[...]
    et[:, :, voc:] = jnp.zeros((2, dim, et.shape[2] - voc), BF16)
    dz[:, voc:, :] = jnp.zeros((2, dz.shape[1] - voc, dz.shape[2]), BF16)

    pl.semaphore_wait(barrier, ndev - 1)

    ways = (plus, minus)
    back = (minus, plus)

    def first(g, k, dmin=0):
        s = xslot(g, 0, dmin)
        return rcopy(s, s, ag1_s.at[g, 0, k], ag1_r.at[g, 0, k], dev(g, 0, ways[k]))

    def first_fwd(g, k, dmin):
        s = xslot(g, 0, dmin, k * (half // 2), half // 2)
        return rcopy(s, s, ag1_s.at[g, 1, k], ag1_r.at[g, 1, k], dev(g, 0, ways[k]))

    rel_pos = (0, minus, plus, 2)

    def second(g, r, k, dmaj=0):
        s = xslot(g, dmaj, rel_pos[r])
        return rcopy(s, s, ag2_s.at[g, r, k], ag2_r.at[g, r, k], dev(g, ways[k], 0))

    def third(g, r, dmaj):
        s = xslot(g, dmaj, rel_pos[r])
        return rcopy(s, s, ag3_s.at[g, r], ag3_r.at[g, r], dev(g, ways[r // 2], 0))

    def to_peers(ref, ssem, rsem):
        out = []
        for d in range(1, chips):
            out.append(rcopy(ref, ref, ssem.at[d], rsem.at[d], {"tp": lax.rem(chip + d, chips) * CORES + core}))
            out[-1].start()
        return out

    def from_peers(ref_of, ssem, rsem):
        for d in range(1, chips):
            s = ref_of(lax.rem(chip + chips - d, chips))
            rcopy(s, s, ssem.at[d], rsem.at[d], {"tp": sib}).wait_recv()

    tms = to_peers(tm_all.at[chip], tm_s, tm_r)
    for g in PAIR:
        for k in PAIR:
            first(g, k).start()
    e_send = rcopy(emb_ref, ee.at[1], pr_s.at[0], pr_r.at[0], {"tp": sib})
    e_send.start()
    for g in PAIR:
        for k in PAIR:
            second(g, 0, k).start()

    for k in PAIR:
        for g in PAIR:
            first(g, k, back[k]).wait_recv()
            first_fwd(g, k, back[k]).start()
    for k in PAIR:
        for g in PAIR:
            for j in PAIR:
                second(g, 1 + k, j).start()

    def transpose_e(h):
        for r0, n in row_tiles(voc, 384):
            et[h, :, r0:r0 + n] = ee[h, r0:r0 + n, :].T

    loads[-1].wait()
    transpose_e(0)
    for g in PAIR:
        for k in PAIR:
            second(g, 0, k, back[k]).wait_recv()
        third(g, 0, minus).start()
    from_peers(lambda t: tm_all.at[t], tm_s, tm_r)
    for c in range(nck):
        for j in PAIR:
            v = tm_all[2 * c + j]
            tgt_ck[c:c + 1, j * tok:(j + 1) * tok] = v[0:1]
            msk_ck[c:c + 1, j * tok:(j + 1) * tok] = v[1:2]
    rel_ck[0] = tgt_ck[...] - me * voc
    rel_ck[1] = tgt_ck[...] - sib * voc
    maskf = msk_ck[...].astype(F32)
    pair[0] = jnp.broadcast_to(jnp.sum(maskf, keepdims=True), (8, tok))
    cnt_send = rcopy(pair.at[0], pair.at[1], pr_s.at[1], pr_r.at[1], {"tp": sib})
    cnt_send.start()
    e_send.wait_recv()
    transpose_e(1)

    tiles = [(h, r0, n) for h in PAIR for r0, n in row_tiles(voc, TILE)]

    def chunk_at(dy, dj):
        y, j = lax.rem(my + dy, side), lax.rem(mx // 2 + dj, pairs)
        return y * pairs + j, y, pl.multiple_of(j * ct, ct)

    def logits_chunk(dy, dj):
        c, i, lane0 = chunk_at(dy, dj)
        x_c = xg[pl.ds(pl.multiple_of(c * ct, ct), ct), :]
        top = None
        for h, r0, n in tiles:
            z = lax.dot_general(ee[h, r0:r0 + n, :], x_c, NT, preferred_element_type=F32)
            ez[i, h, r0:r0 + n, pl.ds(lane0, ct)] = z
            t = jnp.max(z, axis=0, keepdims=True)
            top = t if top is None else jnp.maximum(top, t)
        tot = jnp.zeros((1, ct), F32)
        tl = jnp.zeros((1, ct), F32)
        for h, r0, n in tiles:
            z = ez[i, h, r0:r0 + n, pl.ds(lane0, ct)]
            e = jnp.exp(z - top)
            ez[i, h, r0:r0 + n, pl.ds(lane0, ct)] = e
            tot += jnp.sum(e, axis=0, keepdims=True)
            hit = lax.broadcasted_iota(jnp.int32, (n, ct), 0) == rel_ck[h, pl.ds(c, 1), :] - r0
            tl += jnp.sum(jnp.where(hit, z, 0.0), axis=0, keepdims=True)
        top_ck[pl.ds(c, 1), :] = top
        tl_all[chip, pl.ds(c, 1), :] = tl
        st_all[c, chip] = top + jnp.log(tot)
        to_peers(st_all.at[c, chip], st_s.at[c], st_r.at[c])

    def gather1():
        for g in PAIR:
            for r in (1, 2):
                for k in PAIR:
                    second(g, r, k, back[k]).wait_recv()
                third(g, r, back[r // 2]).start()
        for g in PAIR:
            for k in PAIR:
                first_fwd(g, k, 2).wait_recv()
            for j in PAIR:
                second(g, 3, j).start()

    def gather3():
        for g in PAIR:
            third(g, 0, 2).wait_recv()

    def gather4():
        for g in PAIR:
            for k in PAIR:
                second(g, 3, k, back[k]).wait_recv()
            third(g, 3, plus).start()
        for g in PAIR:
            for r in (1, 2):
                third(g, r, 2).wait_recv()

    def gather7():
        for g in PAIR:
            third(g, 3, 2).wait_recv()

    def logits_step(k, carry):
        for i, event in ((1, gather1), (3, gather3), (4, gather4), (7, gather7)):
            pl.when(k == i)(event)
        far, t = k // 6, lax.rem(k, 3)
        logits_chunk((t + t // 2) * (1 - far) + 2 * far, (k // 3) * (1 - far) + (k - 6) * far)
        return carry

    lax.fori_loop(0, nck, logits_step, 0)
    tls = to_peers(tl_all.at[chip], tl_s, tl_r)
    cnt_send.wait_recv()
    total_n = (pair[0] + pair[1])[0:1, 0:1]
    s_ck[...] = maskf / total_n

    def grad_chunk(dy, dj):
        c, i, lane0 = chunk_at(dy, dj)
        out0 = pl.multiple_of(c * ct, ct)
        from_peers(lambda t: st_all.at[c, t], st_s.at[c], st_r.at[c])
        part = st_all[c]
        top = jnp.max(part, axis=0)
        lse = top + jnp.log(jnp.sum(jnp.exp(part - top[None]), axis=0))
        lse_ck[pl.ds(c, 1), :] = lse
        s = s_ck[pl.ds(c, 1), :]
        a = jnp.exp(top_ck[pl.ds(c, 1), :] - lse) * s
        for h, r0, n in tiles:
            e = ez[i, h, r0:r0 + n, pl.ds(lane0, ct)]
            hit = lax.broadcasted_iota(jnp.int32, (n, ct), 0) == rel_ck[h, pl.ds(c, 1), :] - r0
            dz[h, r0:r0 + n, pl.ds(out0, ct)] = (e * a - jnp.where(hit, s, 0.0)).astype(BF16)
        for q in PAIR:
            acc = None
            for h in PAIR:
                t = lax.dot_general(et[h, q * hd:(q + 1) * hd, :], dz[h, :, pl.ds(out0, ct)], NN,
                                    preferred_element_type=F32)
                acc = t if acc is None else acc + t
            for j in PAIR:
                dxp[2 * c + j, q * hd:(q + 1) * hd, :] = acc[:, j * tok:(j + 1) * tok]

    hops = ((2, 0, 0, minus), (2, 1, 1, plus), (plus, 0, 1, plus), (minus, 1, 2, minus), (minus, 0, 0, minus), (plus, 1, 3, plus))

    def part(g, dmaj, dmin, q):
        return chip_at(*rel(g, dmaj, dmin)), pl.ds(g * hd + q * qd, qd)

    def ring1(g, s, k, hop=None):
        d, q, slot, to = hop or hops[k]
        src = dxp.at[chip_at(*rel(g, d, s)), pl.ds(g * hd + q * qd, qd)]
        land = r2 if hop or k > 1 else r1
        return rcopy(src, land.at[g, s, slot], rs_s.at[g, s, k], rs_r.at[g, s, k], dev(g, to, 0))

    def direct1(g, s, b):
        ring1(g, s, 2 + b, (1 + 2 * b, b, 1 + b, 1 + 2 * b)).start()

    def relay1(g, s):
        for k in PAIR:
            ring1(g, s, k).wait_recv()
            i, q = part(g, ways[1 - k], s, k)
            dxp[i, q, :] = dxp[i, q, :] + r1[g, s, k]
            ring1(g, s, k + 4).start()

    def ring2(g, k):
        d, q, slot, to = hops[k]
        src = dxp.at[chip_at(*rel(g, 0, d)), pl.ds(g * hd + q * qd, qd)]
        return rcopy(src, (q1 if k < 2 else q2).at[g, slot], ring_s.at[g, k], ring_r.at[g, k], dev(g, 0, to))

    def finish1(s):
        for g in PAIR:
            for k in range(2, 6):
                ring1(g, s, k).wait_recv()
            for q in PAIR:
                i, rows = part(g, 0, s, q)
                dxp[i, rows, :] = dxp[i, rows, :] + r2[g, s, 2 * q] + r2[g, s, 2 * q + 1]
            for k in {2: PAIR, plus: (2,), minus: (3,), 0: ()}[s]:
                ring2(g, k).start()

    def relay2():
        for k in PAIR:
            for g in PAIR:
                ring2(g, k).wait_recv()
                i, q = part(g, 0, ways[1 - k], k)
                dxp[i, q, :] = dxp[i, q, :] + q1[g, k]
                ring2(g, k + 4).start()

    near, far = 1 + 2 * odd, 3 - 2 * odd

    def grad_step(dy, dj):
        grad_chunk(dy, dj)
        for s in (2, far) if dj else (0, near):
            for k in {2: PAIR, plus: (2,), minus: (3,), 0: ()}[dy]:
                ring1(0, s, k).start()
        if dj:
            for k in PAIR:
                ring1(1, dy, k).start()
        direct1(1, dy, 1 - odd if dj else odd)

    grad_step(2, 1)
    grad_step(2, 0)
    grad_step(plus, 1)
    grad_step(minus, 1)
    relay1(0, 2)
    relay1(0, far)
    relay1(1, 2)
    grad_step(0, 1)
    grad_step(plus, 0)
    grad_step(minus, 0)
    relay1(0, near)
    relay1(1, plus)
    relay1(1, minus)
    relay1(0, 0)
    grad_step(0, 0)
    relay1(1, 0)
    pl.semaphore_signal(free_sem, inc=1, device_id={"tp": sib}, device_id_type=MESH)

    def embed_grad(h, dst, t):
        r0, n = row_tiles(voc, 528)[t]
        ez[0, dst, r0:r0 + n, :] = lax.dot_general(dz[h, r0:r0 + n, :], xg[...], NN, preferred_element_type=F32)

    for t in range(3):
        embed_grad(1, 0, t)
    pl.semaphore_wait(free_sem, 1)
    de_send = rcopy(ez.at[0, 0], ez.at[1, 0], pr_s.at[3], pr_r.at[3], {"tp": sib})
    de_send.start()

    from_peers(lambda t: tl_all.at[t], tl_s, tl_r)
    loss = (lse_ck[...] - jnp.sum(tl_all[...], axis=0)) * maskf
    loss_ck[...] = loss
    pair[2] = jnp.broadcast_to(jnp.sum(loss, keepdims=True), (8, tok))
    loss_send = rcopy(pair.at[2], pair.at[3], pr_s.at[2], pr_r.at[2], {"tp": sib})
    loss_send.start()

    finish1(2)
    embed_grad(0, 1, 0)
    finish1(plus)
    finish1(minus)
    embed_grad(0, 1, 1)
    relay2()
    finish1(0)
    embed_grad(0, 1, 2)
    de_send.wait_recv()
    for r0, n in row_tiles(voc, 528):
        ez[0, 1, r0:r0 + n, :] = ez[0, 1, r0:r0 + n, :] + ez[1, 0, r0:r0 + n, :]
    de_out = pltpu.make_async_copy(ez.at[0, 1], dE_out, out_sem.at[0])
    de_out.start()
    loss_send.wait_recv()
    sm_buf[...] = (pair[2] + pair[3]) / total_n
    row = loss_ck[pl.ds(chip // 2, 1), :]
    sm_buf[0:1, :] = jnp.where(odd == 0, row[:, :tok], row[:, tok:])
    sm_copy = pltpu.make_async_copy(sm_buf, sm_out, out_sem.at[1])
    sm_copy.start()

    for g in PAIR:
        for k in range(2, 6):
            ring2(g, k).wait_recv()

    own = [dxp[chip, (2 * g + q) * qd:(2 * g + q + 1) * qd, :] + q2[g, 2 * q] + q2[g, 2 * q + 1] for g in PAIR for q in PAIR]
    dx = jnp.concatenate([v.T for v in own], axis=1)
    normed, rstd = normalize()
    dgam = jnp.sum(dx * normed, axis=0, keepdims=True)
    dbet = jnp.sum(dx, axis=0, keepdims=True)
    quarter = dim // tok
    for j in range(quarter):
        dl_all[me, j:j + 1, :] = dgam[:, j * tok:(j + 1) * tok]
        dl_all[me, quarter + j:quarter + j + 1, :] = dbet[:, j * tok:(j + 1) * tok]
    dls = []
    for d in range(1, ndev):
        cp = rcopy(dl_all.at[me], dl_all.at[me], dl_s.at[d], dl_r.at[d], {"tp": lax.rem(me + d, ndev)})
        cp.start()
        dls.append(cp)
    dn = dx * lnp_ref[0:1, :]
    dh = rstd * (dn - jnp.mean(dn, axis=-1, keepdims=True) - normed * jnp.mean(dn * normed, axis=-1, keepdims=True))
    dh_buf[...] = dh.astype(BF16)
    dh_copy = pltpu.make_async_copy(dh_buf, dh_out, out_sem.at[2])
    dh_copy.start()

    for g in PAIR:
        for k in PAIR:
            first(g, k).wait_send()
            first_fwd(g, k, back[k]).wait_send()
        for r in range(4):
            for k in PAIR:
                second(g, r, k).wait_send()
            third(g, r, back[r // 2]).wait_send()
        for k in range(6):
            for s in range(side):
                ring1(g, s, k).wait_send()
            ring2(g, k).wait_send()
    for c in range(nck):
        for d in range(1, chips):
            rcopy(st_all.at[c, chip], st_all.at[c, chip], st_s.at[c, d], st_r.at[c, d], {"tp": sib}).wait_send()
    for cp in tms + tls + [e_send, cnt_send, de_send, loss_send]:
        cp.wait_send()

    for d in range(1, ndev):
        s = dl_all.at[lax.rem(me + ndev - d, ndev)]
        rcopy(s, s, dl_s.at[d], dl_r.at[d], {"tp": sib}).wait_recv()
    dl = jnp.sum(dl_all[...], axis=0)
    for j in range(quarter):
        for i in PAIR:
            dln_buf[i:i + 1, j * tok:(j + 1) * tok] = dl[i * quarter + j:i * quarter + j + 1]
    dln_copy = pltpu.make_async_copy(dln_buf, dln_out, out_sem.at[3])
    dln_copy.start()
    for cp in dls:
        cp.wait_send()
    for cp in (de_out, sm_copy, dh_copy, dln_copy):
        cp.wait()


def adam_kernel(*refs):
    big_in, small_in = refs[:4], refs[4:10]
    e_new, m1_new, m2_new, ln_new, lm1_new, lm2_new, loss_o, mean_o, dh_o = refs[10:19]
    scratch = refs[19:]
    big_buf, small_buf, big_res, ln_res, loss_res, mean_res = scratch[:4], scratch[4:10], scratch[10:13], scratch[13:16], scratch[16], scratch[17]
    in_sem, small_sem, out_sem, sout_sem = scratch[18:]
    tiles = row_tiles(big_in[0].shape[0], 272)
    small = [pltpu.make_async_copy(s, d, small_sem.at[i]) for i, (s, d) in enumerate(zip(small_in, small_buf))]
    reads = [[pltpu.make_async_copy(s.at[pl.ds(r0, n)], d.at[pl.ds(r0, n)], in_sem.at[t, i])
              for i, (s, d) in enumerate(zip(big_in, big_buf))] for t, (r0, n) in enumerate(tiles)]
    for cp in reads[0] + small:
        cp.start()
    for row in reads[1:]:
        for cp in row:
            cp.start()
    writes = []
    for t, (r0, n) in enumerate(tiles):
        for cp in reads[t]:
            cp.wait()
        sl = slice(r0, r0 + n)
        grad, emb, m1, m2 = [b[sl, :] for b in big_buf]
        res = adam_step(emb.astype(F32), grad, m1, m2, WEIGHT_DECAY)
        for i, (buf, dst, val) in enumerate(zip(big_res, (e_new, m1_new, m2_new), res)):
            buf[sl, :] = val.astype(buf.dtype)
            writes.append(pltpu.make_async_copy(buf.at[pl.ds(r0, n)], dst.at[pl.ds(r0, n)], out_sem.at[t, i]))
            writes[-1].start()
    for cp in small:
        cp.wait()
    dln, lnp, lm1, lm2, sm, dh = small_buf
    for buf, val in zip(ln_res, adam_step(lnp[...], dln[...], lm1[...], lm2[...], 0.0)):
        buf[...] = val
    loss_res[...] = sm[0:1, :]
    mean_res[...] = sm[1:2, 0:1]
    for i, (src, dst) in enumerate(zip((*ln_res, loss_res, mean_res, dh), (ln_new, lm1_new, lm2_new, loss_o, mean_o, dh_o))):
        writes.append(pltpu.make_async_copy(src, dst, sout_sem.at[i]))
        writes[-1].start()
    for cp in writes:
        cp.wait()


def solution(mesh):
    ntp = mesh.shape["tp"]
    side = math.isqrt(ntp // CORES)
    row_spec = P(("dp", "tp"), None)
    tok_spec = P(("dp", "tp"))
    vocab_spec = P("tp", None)
    repl_spec = P()
    part_spec = P("dp", None)

    def device_step(hidden, targets, loss_mask, ln_params, out_embed, ln_mom1, ln_mom2, embed_mom1, embed_mom2):
        tok, dim = hidden.shape
        voc = out_embed.shape[0]
        half, chips = tok // 2, side * side
        ct, nck, qd = 2 * tok, chips // 2, dim // 4
        ntok = ct * nck
        vpad = -(-voc // 128) * 128
        dma, vm = pltpu.SemaphoreType.DMA, pltpu.VMEM
        big, sem2 = jax.ShapeDtypeStruct((voc, dim), F32), [dma((2, 2, 2))] * 2
        ln_s, sm_s = jax.ShapeDtypeStruct((2, dim), F32), jax.ShapeDtypeStruct((8, tok), F32)
        dh_s = jax.ShapeDtypeStruct((tok, dim), BF16)
        dE, dh, dln, sm = pl.pallas_call(
            functools.partial(step_kernel, side),
            out_shape=[big, dh_s, ln_s, sm_s],
            in_specs=[ANY] * 5,
            out_specs=[ANY] * 4,
            scratch_shapes=[
                vm((tok, dim), BF16), *[vm((1, tok), jnp.int32)] * 2, vm((2, dim), F32),
                vm((tok, dim), BF16), vm((2, dim), F32), vm((8, tok), F32),
                vm((ntok, dim), BF16),
                vm((2, voc, dim), BF16),
                vm((2, dim, vpad), BF16),
                vm((nck // 2, 2, voc, 2 * ct), F32),
                vm((2, vpad, ntok), BF16),
                vm((chips, dim, tok), F32),
                vm((2, side, 2, qd, tok), F32),
                vm((2, side, 4, qd, tok), F32),
                vm((2, 2, qd, tok), F32),
                vm((2, 4, qd, tok), F32),
                vm((chips, 2, tok), jnp.int32),
                vm((nck, chips, 1, ct), F32),
                vm((chips, nck, ct), F32),
                *[vm((nck, ct), jnp.int32)] * 2, vm((2, nck, ct), jnp.int32),
                *[vm((nck, ct), F32)] * 4,
                vm((4, 8, tok), F32),
                vm((ntp, 8, tok), F32),
                dma((5,)), dma((4,)), *sem2, *[dma((2, 4, 2))] * 2, *[dma((2, 4))] * 2,
                *[dma((chips,))] * 2, *[dma((nck, chips))] * 2, *[dma((chips,))] * 2,
                *[dma((2, side, 6))] * 2, *[dma((2, 6))] * 2, *[dma((ntp,))] * 2, *[dma((4,))] * 2,
                pltpu.SemaphoreType.REGULAR,
            ],
            compiler_params=pltpu.CompilerParams(collective_id=0, has_side_effects=True, vmem_limit_bytes=67043328),
            name="head_step",
        )(hidden, targets.reshape(1, tok), loss_mask.reshape(1, tok), ln_params, out_embed)

        big_b, nt = jax.ShapeDtypeStruct((voc, dim), BF16), len(row_tiles(voc, 272))
        shapes = [big, big_b, big, big, ln_s, ln_s, ln_s, ln_s, sm_s, dh_s]
        outs = [big_b, big, big, ln_s, ln_s, ln_s, jax.ShapeDtypeStruct((1, tok), F32), jax.ShapeDtypeStruct((1, 1), F32), dh_s]
        e_new, m1n, m2n, lnn, lm1n, lm2n, loss, mean, dh = pl.pallas_call(
            adam_kernel,
            out_shape=outs,
            in_specs=[ANY] * len(shapes),
            out_specs=[ANY] * len(outs),
            scratch_shapes=[vm(s.shape, s.dtype) for s in shapes + outs[:8]]
            + [dma((nt, 4)), dma((6,)), dma((nt, 3)), dma((6,))],
            compiler_params=pltpu.CompilerParams(vmem_limit_bytes=67043328),
            name="adam_step",
        )(dE, out_embed, embed_mom1, embed_mom2, dln, ln_params, ln_mom1, ln_mom2, sm, dh)
        return (loss.reshape(tok), mean.reshape(1), dh, lnn, lm1n, lm2n, e_new, m1n, m2n)

    return jax.shard_map(device_step, mesh=mesh, in_specs=(row_spec, tok_spec, tok_spec, repl_spec, vocab_spec, repl_spec, repl_spec, vocab_spec, vocab_spec), out_specs=(tok_spec, P("dp"), row_spec, part_spec, part_spec, part_spec, row_spec, row_spec, row_spec), check_vma=False)
```

time: 365 us -> 83.4 us (0.23)
  blocking collectives: 204 us -> 0 us
  Pallas kernels: 0 us -> 82.4 us
  waiting for transfers between devices: 64 us -> 0 us
  matrix products: 40.4 us -> 0 us
  other arithmetic: 33.2 us -> 0 us
  between operations: 16.7 us -> 0.83 us
  local copies, waits for them, and re-layouts: 6.02 us -> 0 us
    psum x2 -> x0, blocking collectives: 91.5 us -> none  [the longest x1 46.5 us: device_step(): d_ln = lax.psum(d_ln, 'tp')]
    pallas_call x0 -> x2, Pallas kernels: none -> 82.4 us  [the longest x1 74.3 us: device_step(): pl.pallas_call(functools.partial(step_kernel, side), out_shape=[big, dh_s...]
    all_gather x2 -> x0, blocking collectives: 64 us -> none  [the longest x1 32.3 us: device_step(): tgt_full = lax.all_gather(targets, 'tp', tiled=True)]
    reduce_scatter x1 -> x0, waiting for transfers between devices: 63.9 us -> none  [device_step(): d_x = lax.psum_scatter(d_x_part, 'tp', scatter_dimension=0, tiled=True)]
    pmax x1 -> x0, blocking collectives: 48.4 us -> none  [device_step(): global_max = lax.pmax(local_max, 'tp')]
    dot_general x3 -> x0, matrix products: 40.4 us -> none  [the longest x1 16 us: device_step(): lax.dot_general(d_logits, x_full, (((0,), (0,)), ((), ())), preferred_ele...]
    reduce_sum x7 -> x0, other arithmetic: 18.1 us -> none  [the longest x1 11.8 us: device_step(): local_sum = jnp.sum(jnp.exp(logits - local_max[:, None]), axis=1)]
    convert_element_type x4 -> x0, other arithmetic: 14.4 us -> none  [the longest x1 11.9 us: device_step(): ((jnp.exp(logits - log_norm[:, None]) - is_target.astype(jnp.float32)) *...]
  transfers between devices with their start and end apart: 2 -> 0, of which waited for: 1 -> 0; matrix products, arithmetic and copies ran while one was open for 5% -> 0% of each run, Pallas kernels for 0% -> 0%
where the time goes in v2:
time: 83.4 us; the launch traced here: 83.3 us
  Pallas kernels  82.4 us (99%)
    pallas_call x1, Pallas kernels, device_step(): pl.pallas_call(functools.partial(step_kernel, side), out_shape=[big, dh_s...  74.3 us
    pallas_call x1, Pallas kernels, device_step(): pl.pallas_call(adam_kernel, out_shape=outs, in_specs=[ANY] * len(shapes),...  8.16 us

profile of v2, /device:TPU:97, one launch (start us, length us, event | category | flops | bytes accessed | tf_op | source)
XLA Modules:
  0.0 83.3 jit_solution(5031620689587963927)
XLA Ops:
  0.6 74.3 %head_step.1 = (f32[1572,512]{1,0:T(8,128)}, bf16[128,512]{1,0:T(8,128)(2,1)}, f32[2,512]{1,0:T(2,128)}, f32[8,128]{1,0:T(8,128)}) custom-call(bf16[128,512]{1,0:T(8,128)(2,1)} %hid_hbm.1, s32[1,128]{1,0:T(1,128)} %bitcast.4, s32[1,128]{1,0:T(1,128)} %bitcast.5, f32[2,512]{1,0:T(2,128)} %refs_5_.1, bf16[1572,512]{1,0:T(8,128)(2,1)} %refs_1_.1), custom_call_target="tpu_custom_call" | custom-call | tf_op jit(solution)/shard_map/head_step/pallas_call | solution.py:507
  74.9 8.2 %adam_step.1 = (bf16[1572,512]{1,0:T(8,128)(2,1)}, f32[1572,512]{1,0:T(8,128)}, f32[1572,512]{1,0:T(8,128)}, f32[2,512]{1,0:T(2,128)}, f32[2,512]{1,0:T(2,128)},...) custom-call(f32[1572,512]{1,0:T(8,128)} %get-tuple-element.22.refs_0_, ...), custom_call_target="tpu_custom_call" | custom-call | tf_op jit(solution)/shard_map/adam_step/pallas_call | solution.py:544

commit v3 on v2

--- a/solution.py
+++ b/solution.py
@@ -18,7 +18,7 @@
 MESH = pl.DeviceIdType.MESH
 CORES = 2
 PAIR = (0, 1)
-TILE = 528
+TILE = 320
 ANY = pl.BlockSpec(memory_space=pl.ANY)
 F32, BF16 = jnp.float32, jnp.bfloat16
 NN = (((1,), (0,)), ((), ()))
@@ -42,9 +42,9 @@
                 dE_out, dh_out, dln_out, sm_out,
                 hid_ref, tgt_ref, msk_ref, lnp_ref, dh_buf, dln_buf, sm_buf,
                 xg, ee, et, ez, dz, dxp, r1, r2, q1, q2,
-                tm_all, st_all, tl_all, tgt_ck, msk_ck, rel_ck, top_ck, lse_ck, s_ck, loss_ck, pair, dl_all,
-                in_sem, out_sem, ag1_s, ag1_r, ag2_s, ag2_r, ag3_s, ag3_r, tm_s, tm_r, st_s, st_r, tl_s, tl_r,
-                rs_s, rs_r, ring_s, ring_r, dl_s, dl_r, pr_s, pr_r, free_sem):
+                tm_all, st_all, tl_all, zb, tgt_ck, msk_ck, rel_ck, top_ck, lse_ck, s_ck, loss_ck, pair, dl_all,
+                in_sem, out_sem, ag_s, ag1_r, ag2_r, ag3_r, tm_s, tm_r, st_s, st_r, tl_s, tl_r,
+                rs_s, rs_r, ring_r, dl_s, dl_r, pr_s, pr_r, free_sem):
     chips = side * side
     ndev = chips * CORES
     tok, dim = hid_ref.shape
@@ -110,35 +110,31 @@
 
     def first(g, k, dmin=0):
         s = xslot(g, 0, dmin)
-        return rcopy(s, s, ag1_s.at[g, 0, k], ag1_r.at[g, 0, k], dev(g, 0, ways[k]))
+        return rcopy(s, s, ag_s, ag1_r.at[g, 0, k], dev(g, 0, ways[k]))
 
     def first_fwd(g, k, dmin):
         s = xslot(g, 0, dmin, k * (half // 2), half // 2)
-        return rcopy(s, s, ag1_s.at[g, 1, k], ag1_r.at[g, 1, k], dev(g, 0, ways[k]))
+        return rcopy(s, s, ag_s, ag1_r.at[g, 1, k], dev(g, 0, ways[k]))
 
     rel_pos = (0, minus, plus, 2)
 
     def second(g, r, k, dmaj=0):
         s = xslot(g, dmaj, rel_pos[r])
-        return rcopy(s, s, ag2_s.at[g, r, k], ag2_r.at[g, r, k], dev(g, ways[k], 0))
+        return rcopy(s, s, ag_s, ag2_r.at[g, r, k], dev(g, ways[k], 0))
 
     def third(g, r, dmaj):
         s = xslot(g, dmaj, rel_pos[r])
-        return rcopy(s, s, ag3_s.at[g, r], ag3_r.at[g, r], dev(g, ways[r // 2], 0))
+        return rcopy(s, s, ag_s, ag3_r.at[g, r], dev(g, ways[r // 2], 0))
 
     def to_peers(ref, ssem, rsem):
-        out = []
         for d in range(1, chips):
-            out.append(rcopy(ref, ref, ssem.at[d], rsem.at[d], {"tp": lax.rem(chip + d, chips) * CORES + core}))
-            out[-1].start()
-        return out
-
-    def from_peers(ref_of, ssem, rsem):
-        for d in range(1, chips):
-            s = ref_of(lax.rem(chip + chips - d, chips))
-            rcopy(s, s, ssem.at[d], rsem.at[d], {"tp": sib}).wait_recv()
-
-    tms = to_peers(tm_all.at[chip], tm_s, tm_r)
+            rcopy(ref, ref, ssem, rsem, {"tp": lax.rem(chip + d, chips) * CORES + core}).start()
+
+    def all_of(ref, ssem, rsem):
+        return rcopy(ref, ref, ssem, rsem, {"tp": sib})
+
+    to_peers(tm_all.at[chip], tm_s, tm_r)
+    tms = all_of(tm_all.at[pl.ds(0, chips - 1)], tm_s, tm_r)
     for g in PAIR:
         for k in PAIR:
             first(g, k).start()
@@ -167,7 +163,7 @@
         for k in PAIR:
             second(g, 0, k, back[k]).wait_recv()
         third(g, 0, minus).start()
-    from_peers(lambda t: tm_all.at[t], tm_s, tm_r)
+    tms.wait_recv()
     for c in range(nck):
         for j in PAIR:
             v = tm_all[2 * c + j]
@@ -191,25 +187,32 @@
     def logits_chunk(dy, dj):
         c, i, lane0 = chunk_at(dy, dj)
         x_c = xg[pl.ds(pl.multiple_of(c * ct, ct), ct), :]
-        top = None
-        for h, r0, n in tiles:
+        tops, tots = [], []
+        tl = jnp.zeros((1, ct), F32)
+
+        def finish_tile(t):
+            h, r0, n = tiles[t]
+            z = zb[t % 2, :n, :]
+            e = jnp.exp(z - tops[t])
+            ez[i, h, r0:r0 + n, pl.ds(lane0, ct)] = e
+            tots.append(jnp.sum(e, axis=0, keepdims=True))
+            hit = lax.broadcasted_iota(jnp.int32, (n, ct), 0) == rel_ck[h, pl.ds(c, 1), :] - r0
+            return jnp.sum(jnp.where(hit, z, 0.0), axis=0, keepdims=True)
+
+        for t, (h, r0, n) in enumerate(tiles):
             z = lax.dot_general(ee[h, r0:r0 + n, :], x_c, NT, preferred_element_type=F32)
-            ez[i, h, r0:r0 + n, pl.ds(lane0, ct)] = z
-            t = jnp.max(z, axis=0, keepdims=True)
-            top = t if top is None else jnp.maximum(top, t)
-        tot = jnp.zeros((1, ct), F32)
-        tl = jnp.zeros((1, ct), F32)
-        for h, r0, n in tiles:
-            z = ez[i, h, r0:r0 + n, pl.ds(lane0, ct)]
-            e = jnp.exp(z - top)
-            ez[i, h, r0:r0 + n, pl.ds(lane0, ct)] = e
-            tot += jnp.sum(e, axis=0, keepdims=True)
-            hit = lax.broadcasted_iota(jnp.int32, (n, ct), 0) == rel_ck[h, pl.ds(c, 1), :] - r0
-            tl += jnp.sum(jnp.where(hit, z, 0.0), axis=0, keepdims=True)
-        top_ck[pl.ds(c, 1), :] = top
+            zb[t % 2, :n, :] = z
+            tops.append(jnp.max(z, axis=0, keepdims=True))
+            if t:
+                tl += finish_tile(t - 1)
+        tl += finish_tile(len(tiles) - 1)
+        top = functools.reduce(jnp.maximum, tops)
+        tot = sum(s * jnp.exp(m - top) for m, s in zip(tops, tots))
+        for t, m in enumerate(tops):
+            top_ck[t, pl.ds(c, 1), :] = m
         tl_all[chip, pl.ds(c, 1), :] = tl
         st_all[c, chip] = top + jnp.log(tot)
-        to_peers(st_all.at[c, chip], st_s.at[c], st_r.at[c])
+        to_peers(st_all.at[c, chip], st_s, st_r.at[c])
 
     def gather1():
         for g in PAIR:
@@ -248,7 +251,8 @@
         return carry
 
     lax.fori_loop(0, nck, logits_step, 0)
-    tls = to_peers(tl_all.at[chip], tl_s, tl_r)
+    to_peers(tl_all.at[chip], tl_s, tl_r)
+    tls = all_of(tl_all.at[pl.ds(0, chips - 1)], tl_s, tl_r)
     cnt_send.wait_recv()
     total_n = (pair[0] + pair[1])[0:1, 0:1]
     s_ck[...] = maskf / total_n
@@ -256,14 +260,14 @@
     def grad_chunk(dy, dj):
         c, i, lane0 = chunk_at(dy, dj)
         out0 = pl.multiple_of(c * ct, ct)
-        from_peers(lambda t: st_all.at[c, t], st_s.at[c], st_r.at[c])
+        all_of(st_all.at[c, pl.ds(0, chips - 1)], st_s, st_r.at[c]).wait_recv()
         part = st_all[c]
         top = jnp.max(part, axis=0)
         lse = top + jnp.log(jnp.sum(jnp.exp(part - top[None]), axis=0))
         lse_ck[pl.ds(c, 1), :] = lse
         s = s_ck[pl.ds(c, 1), :]
-        a = jnp.exp(top_ck[pl.ds(c, 1), :] - lse) * s
-        for h, r0, n in tiles:
+        for t, (h, r0, n) in enumerate(tiles):
+            a = jnp.exp(top_ck[t, pl.ds(c, 1), :] - lse) * s
             e = ez[i, h, r0:r0 + n, pl.ds(lane0, ct)]
             hit = lax.broadcasted_iota(jnp.int32, (n, ct), 0) == rel_ck[h, pl.ds(c, 1), :] - r0
             dz[h, r0:r0 + n, pl.ds(out0, ct)] = (e * a - jnp.where(hit, s, 0.0)).astype(BF16)
@@ -285,7 +289,7 @@
         d, q, slot, to = hop or hops[k]
         src = dxp.at[chip_at(*rel(g, d, s)), pl.ds(g * hd + q * qd, qd)]
         land = r2 if hop or k > 1 else r1
-        return rcopy(src, land.at[g, s, slot], rs_s.at[g, s, k], rs_r.at[g, s, k], dev(g, to, 0))
+        return rcopy(src, land.at[g, s, slot], rs_s, rs_r.at[g, s, 2 if hop or k > 1 else k], dev(g, to, 0))
 
     def direct1(g, s, b):
         ring1(g, s, 2 + b, (1 + 2 * b, b, 1 + b, 1 + 2 * b)).start()
@@ -300,12 +304,11 @@
     def ring2(g, k):
         d, q, slot, to = hops[k]
         src = dxp.at[chip_at(*rel(g, 0, d)), pl.ds(g * hd + q * qd, qd)]
-        return rcopy(src, (q1 if k < 2 else q2).at[g, slot], ring_s.at[g, k], ring_r.at[g, k], dev(g, 0, to))
+        return rcopy(src, (q1 if k < 2 else q2).at[g, slot], rs_s, ring_r.at[g, min(k, 2)], dev(g, 0, to))
 
     def finish1(s):
         for g in PAIR:
-            for k in range(2, 6):
-                ring1(g, s, k).wait_recv()
+            all_of(r2.at[g, s], rs_s, rs_r.at[g, s, 2]).wait_recv()
             for q in PAIR:
                 i, rows = part(g, 0, s, q)
                 dxp[i, rows, :] = dxp[i, rows, :] + r2[g, s, 2 * q] + r2[g, s, 2 * q + 1]
@@ -360,7 +363,7 @@
     de_send = rcopy(ez.at[0, 0], ez.at[1, 0], pr_s.at[3], pr_r.at[3], {"tp": sib})
     de_send.start()
 
-    from_peers(lambda t: tl_all.at[t], tl_s, tl_r)
+    tls.wait_recv()
     loss = (lse_ck[...] - jnp.sum(tl_all[...], axis=0)) * maskf
     loss_ck[...] = loss
     pair[2] = jnp.broadcast_to(jnp.sum(loss, keepdims=True), (8, tok))
@@ -388,8 +391,7 @@
     sm_copy.start()
 
     for g in PAIR:
-        for k in range(2, 6):
-            ring2(g, k).wait_recv()
+        all_of(q2.at[g], rs_s, ring_r.at[g, 2]).wait_recv()
 
     own = [dxp[chip, (2 * g + q) * qd:(2 * g + q + 1) * qd, :] + q2[g, 2 * q] + q2[g, 2 * q + 1] for g in PAIR for q in PAIR]
     dx = jnp.concatenate([v.T for v in own], axis=1)
@@ -400,46 +402,30 @@
     for j in range(quarter):
         dl_all[me, j:j + 1, :] = dgam[:, j * tok:(j + 1) * tok]
         dl_all[me, quarter + j:quarter + j + 1, :] = dbet[:, j * tok:(j + 1) * tok]
-    dls = []
     for d in range(1, ndev):
-        cp = rcopy(dl_all.at[me], dl_all.at[me], dl_s.at[d], dl_r.at[d], {"tp": lax.rem(me + d, ndev)})
-        cp.start()
-        dls.append(cp)
+        rcopy(dl_all.at[me], dl_all.at[me], dl_s, dl_r, {"tp": lax.rem(me + d, ndev)}).start()
+    dls = all_of(dl_all.at[pl.ds(0, ndev - 1)], dl_s, dl_r)
     dn = dx * lnp_ref[0:1, :]
     dh = rstd * (dn - jnp.mean(dn, axis=-1, keepdims=True) - normed * jnp.mean(dn * normed, axis=-1, keepdims=True))
     dh_buf[...] = dh.astype(BF16)
     dh_copy = pltpu.make_async_copy(dh_buf, dh_out, out_sem.at[2])
     dh_copy.start()
 
-    for g in PAIR:
-        for k in PAIR:
-            first(g, k).wait_send()
-            first_fwd(g, k, back[k]).wait_send()
-        for r in range(4):
-            for k in PAIR:
-                second(g, r, k).wait_send()
-            third(g, r, back[r // 2]).wait_send()
-        for k in range(6):
-            for s in range(side):
-                ring1(g, s, k).wait_send()
-            ring2(g, k).wait_send()
-    for c in range(nck):
-        for d in range(1, chips):
-            rcopy(st_all.at[c, chip], st_all.at[c, chip], st_s.at[c, d], st_r.at[c, d], {"tp": sib}).wait_send()
-    for cp in tms + tls + [e_send, cnt_send, de_send, loss_send]:
+    blocks = 6 + 16 + 8
+    all_of(xg.at[pl.ds(0, blocks * half)], ag_s, pr_r.at[0]).wait_send()
+    all_of(dxp.at[pl.ds(0, 12 + 3)], rs_s, pr_r.at[0]).wait_send()
+    all_of(st_all.at[:, pl.ds(0, chips - 1)], st_s, pr_r.at[0]).wait_send()
+    for cp in (tms, tls, e_send, cnt_send, de_send, loss_send):
         cp.wait_send()
 
-    for d in range(1, ndev):
-        s = dl_all.at[lax.rem(me + ndev - d, ndev)]
-        rcopy(s, s, dl_s.at[d], dl_r.at[d], {"tp": sib}).wait_recv()
+    dls.wait_recv()
     dl = jnp.sum(dl_all[...], axis=0)
     for j in range(quarter):
         for i in PAIR:
             dln_buf[i:i + 1, j * tok:(j + 1) * tok] = dl[i * quarter + j:i * quarter + j + 1]
     dln_copy = pltpu.make_async_copy(dln_buf, dln_out, out_sem.at[3])
     dln_copy.start()
-    for cp in dls:
-        cp.wait_send()
+    dls.wait_send()
     for cp in (de_out, sm_copy, dh_copy, dln_copy):
         cp.wait()
 
@@ -468,7 +454,7 @@
         res = adam_step(emb.astype(F32), grad, m1, m2, WEIGHT_DECAY)
         for i, (buf, dst, val) in enumerate(zip(big_res, (e_new, m1_new, m2_new), res)):
             buf[sl, :] = val.astype(buf.dtype)
-            writes.append(pltpu.make_async_copy(buf.at[pl.ds(r0, n)], dst.at[pl.ds(r0, n)], out_sem.at[t, i]))
+            writes.append(pltpu.make_async_copy(buf.at[pl.ds(r0, n)], dst.at[pl.ds(r0, n)], out_sem.at[i]))
             writes[-1].start()
     for cp in small:
         cp.wait()
@@ -480,7 +466,9 @@
     for i, (src, dst) in enumerate(zip((*ln_res, loss_res, mean_res, dh), (ln_new, lm1_new, lm2_new, loss_o, mean_o, dh_o))):
         writes.append(pltpu.make_async_copy(src, dst, sout_sem.at[i]))
         writes[-1].start()
-    for cp in writes:
+    for i, buf in enumerate(big_res):
+        pltpu.make_async_copy(buf, (e_new, m1_new, m2_new)[i], out_sem.at[i]).wait()
+    for cp in writes[-6:]:
         cp.wait()
 
 
@@ -501,7 +489,7 @@
         ntok = ct * nck
         vpad = -(-voc // 128) * 128
         dma, vm = pltpu.SemaphoreType.DMA, pltpu.VMEM
-        big, sem2 = jax.ShapeDtypeStruct((voc, dim), F32), [dma((2, 2, 2))] * 2
+        big = jax.ShapeDtypeStruct((voc, dim), F32)
         ln_s, sm_s = jax.ShapeDtypeStruct((2, dim), F32), jax.ShapeDtypeStruct((8, tok), F32)
         dh_s = jax.ShapeDtypeStruct((tok, dim), BF16)
         dE, dh, dln, sm = pl.pallas_call(
@@ -525,13 +513,13 @@
                 vm((chips, 2, tok), jnp.int32),
                 vm((nck, chips, 1, ct), F32),
                 vm((chips, nck, ct), F32),
-                *[vm((nck, ct), jnp.int32)] * 2, vm((2, nck, ct), jnp.int32),
-                *[vm((nck, ct), F32)] * 4,
+                vm((2, TILE, ct), F32), *[vm((nck, ct), jnp.int32)] * 2, vm((2, nck, ct), jnp.int32),
+                vm((2 * len(row_tiles(voc, TILE)), nck, ct), F32), *[vm((nck, ct), F32)] * 3,
                 vm((4, 8, tok), F32),
                 vm((ntp, 8, tok), F32),
-                dma((5,)), dma((4,)), *sem2, *[dma((2, 4, 2))] * 2, *[dma((2, 4))] * 2,
-                *[dma((chips,))] * 2, *[dma((nck, chips))] * 2, *[dma((chips,))] * 2,
-                *[dma((2, side, 6))] * 2, *[dma((2, 6))] * 2, *[dma((ntp,))] * 2, *[dma((4,))] * 2,
+                dma((5,)), dma((4,)), dma(()), dma((2, 2, 2)), dma((2, 4, 2)), dma((2, 4)),
+                dma(()), dma(()), dma(()), dma((nck,)), dma(()), dma(()),
+                dma(()), dma((2, side, 3)), dma((2, 3)), dma(()), dma(()), *[dma((4,))] * 2,
                 pltpu.SemaphoreType.REGULAR,
             ],
             compiler_params=pltpu.CompilerParams(collective_id=0, has_side_effects=True, vmem_limit_bytes=67043328),
@@ -547,7 +535,7 @@
             in_specs=[ANY] * len(shapes),
             out_specs=[ANY] * len(outs),
             scratch_shapes=[vm(s.shape, s.dtype) for s in shapes + outs[:8]]
-            + [dma((nt, 4)), dma((6,)), dma((nt, 3)), dma((6,))],
+            + [dma((nt, 4)), dma((6,)), dma((3,)), dma((6,))],
             compiler_params=pltpu.CompilerParams(vmem_limit_bytes=67043328),
             name="adam_step",
         )(dE, out_embed, embed_mom1, embed_mom2, dln, ln_params, ln_mom1, ln_mom2, sm, dh)

time: 83.4 us -> 76.3 us (0.915)
  Pallas kernels: 82.4 us -> 75.4 us
    pallas_call x1, Pallas kernels: 74.3 us -> 67.4 us  [device_step(): pl.pallas_call(functools.partial(step_kernel, side), out_shape=[big, dh_s...]
where the time goes in v3:
time: 76.3 us; the launch traced here: 76.2 us
  Pallas kernels  75.4 us (99%)
  between operations  0.83 us (1%)
    pallas_call x1, Pallas kernels, device_step(): pl.pallas_call(functools.partial(step_kernel, side), out_shape=[big, dh_s...  67.4 us
    pallas_call x1, Pallas kernels, device_step(): pl.pallas_call(adam_kernel, out_shape=outs, in_specs=[ANY] * len(shapes),...  8.02 us

profile of v3, /device:TPU:97, one launch (start us, length us, event | category | flops | bytes accessed | tf_op | source)
XLA Modules:
  0.0 76.2 jit_solution(5335804722132125397)
XLA Ops:
  0.6 67.4 %head_step.1 = (f32[1572,512]{1,0:T(8,128)}, bf16[128,512]{1,0:T(8,128)(2,1)}, f32[2,512]{1,0:T(2,128)}, f32[8,128]{1,0:T(8,128)}) custom-call(bf16[128,512]{1,0:T(8,128)(2,1)} %hid_hbm.1, s32[1,128]{1,0:T(1,128)} %bitcast.4, s32[1,128]{1,0:T(1,128)} %bitcast.5, f32[2,512]{1,0:T(2,128)} %refs_5_.1, bf16[1572,512]{1,0:T(8,128)(2,1)} %refs_1_.1), custom_call_target="tpu_custom_call" | custom-call | tf_op jit(solution)/shard_map/head_step/pallas_call | solution.py:495
  68.0 8.0 %adam_step.1 = (bf16[1572,512]{1,0:T(8,128)(2,1)}, f32[1572,512]{1,0:T(8,128)}, f32[1572,512]{1,0:T(8,128)}, f32[2,512]{1,0:T(2,128)}, f32[2,512]{1,0:T(2,128)},...) custom-call(f32[1572,512]{1,0:T(8,128)} %get-tuple-element.22.refs_0_, ...), custom_call_target="tpu_custom_call" | custom-call | tf_op jit(solution)/shard_map/adam_step/pallas_call | solution.py:532

commit v4 on v3

--- a/solution.py
+++ b/solution.py
@@ -19,6 +19,7 @@
 CORES = 2
 PAIR = (0, 1)
 TILE = 320
+COPY_TILE = 272
 ANY = pl.BlockSpec(memory_space=pl.ANY)
 F32, BF16 = jnp.float32, jnp.bfloat16
 NN = (((1,), (0,)), ((), ()))
@@ -38,12 +39,12 @@
     return [(r, min(size, rows - r)) for r in range(0, rows, size)]
 
 
-def step_kernel(side, hid_hbm, tgt_hbm, msk_hbm, lnp_hbm, emb_ref,
-                dE_out, dh_out, dln_out, sm_out,
+def step_kernel(side, hid_hbm, tgt_hbm, msk_hbm, lnp_hbm, emb_ref, m1_hbm, m2_hbm,
+                e_out, m1_out, m2_out, dh_out, dln_out, sm_out,
                 hid_ref, tgt_ref, msk_ref, lnp_ref, dh_buf, dln_buf, sm_buf,
                 xg, ee, et, ez, dz, dxp, r1, r2, q1, q2,
                 tm_all, st_all, tl_all, zb, tgt_ck, msk_ck, rel_ck, top_ck, lse_ck, s_ck, loss_ck, pair, dl_all,
-                in_sem, out_sem, ag_s, ag1_r, ag2_r, ag3_r, tm_s, tm_r, st_s, st_r, tl_s, tl_r,
+                in_sem, out_sem, mom_sem, ag_s, ag1_r, ag2_r, ag3_r, tm_s, tm_r, st_s, st_r, tl_s, tl_r,
                 rs_s, rs_r, ring_r, dl_s, dl_r, pr_s, pr_r, free_sem):
     chips = side * side
     ndev = chips * CORES
@@ -335,14 +336,14 @@
                 ring1(1, dy, k).start()
         direct1(1, dy, 1 - odd if dj else odd)
 
+    grad_step(2, 0)
     grad_step(2, 1)
-    grad_step(2, 0)
     grad_step(plus, 1)
     grad_step(minus, 1)
+    grad_step(0, 1)
     relay1(0, 2)
     relay1(0, far)
     relay1(1, 2)
-    grad_step(0, 1)
     grad_step(plus, 0)
     grad_step(minus, 0)
     relay1(0, near)
@@ -350,15 +351,19 @@
     relay1(1, minus)
     relay1(0, 0)
     grad_step(0, 0)
-    relay1(1, 0)
     pl.semaphore_signal(free_sem, inc=1, device_id={"tp": sib}, device_id_type=MESH)
 
     def embed_grad(h, dst, t):
         r0, n = row_tiles(voc, 528)[t]
         ez[0, dst, r0:r0 + n, :] = lax.dot_general(dz[h, r0:r0 + n, :], xg[...], NN, preferred_element_type=F32)
 
-    for t in range(3):
-        embed_grad(1, 0, t)
+    moments = [pltpu.make_async_copy(src, ez.at[2, i], mom_sem.at[i]) for i, src in enumerate((m1_hbm, m2_hbm))]
+    for cp in moments:
+        cp.start()
+    embed_grad(1, 0, 0)
+    relay1(1, 0)
+    embed_grad(1, 0, 1)
+    embed_grad(1, 0, 2)
     pl.semaphore_wait(free_sem, 1)
     de_send = rcopy(ez.at[0, 0], ez.at[1, 0], pr_s.at[3], pr_r.at[3], {"tp": sib})
     de_send.start()
@@ -379,10 +384,19 @@
     finish1(0)
     embed_grad(0, 1, 2)
     de_send.wait_recv()
+    for cp in moments:
+        cp.wait()
+    writes = []
     for r0, n in row_tiles(voc, 528):
-        ez[0, 1, r0:r0 + n, :] = ez[0, 1, r0:r0 + n, :] + ez[1, 0, r0:r0 + n, :]
-    de_out = pltpu.make_async_copy(ez.at[0, 1], dE_out, out_sem.at[0])
-    de_out.start()
+        sl = slice(r0, r0 + n)
+        grad = ez[0, 1, sl, :] + ez[1, 0, sl, :]
+        p, m1, m2 = adam_step(ee[0, sl, :].astype(F32), grad, ez[2, 0, sl, :], ez[2, 1, sl, :], WEIGHT_DECAY)
+        ee[0, sl, :] = p.astype(BF16)
+        ez[2, 0, sl, :] = m1
+        ez[2, 1, sl, :] = m2
+    for i, (src, dst) in enumerate(((ee.at[0], e_out), (ez.at[2, 0], m1_out), (ez.at[2, 1], m2_out))):
+        writes.append(pltpu.make_async_copy(src, dst, mom_sem.at[i]))
+        writes[-1].start()
     loss_send.wait_recv()
     sm_buf[...] = (pair[2] + pair[3]) / total_n
     row = loss_ck[pl.ds(chip // 2, 1), :]
@@ -426,17 +440,17 @@
     dln_copy = pltpu.make_async_copy(dln_buf, dln_out, out_sem.at[3])
     dln_copy.start()
     dls.wait_send()
-    for cp in (de_out, sm_copy, dh_copy, dln_copy):
+    for cp in writes + [sm_copy, dh_copy, dln_copy]:
         cp.wait()
 
 
-def adam_kernel(*refs):
-    big_in, small_in = refs[:4], refs[4:10]
-    e_new, m1_new, m2_new, ln_new, lm1_new, lm2_new, loss_o, mean_o, dh_o = refs[10:19]
-    scratch = refs[19:]
-    big_buf, small_buf, big_res, ln_res, loss_res, mean_res = scratch[:4], scratch[4:10], scratch[10:13], scratch[13:16], scratch[16], scratch[17]
-    in_sem, small_sem, out_sem, sout_sem = scratch[18:]
-    tiles = row_tiles(big_in[0].shape[0], 272)
+def finish_kernel(*refs):
+    big_in, small_in, big_out = refs[:3], refs[3:9], refs[9:12]
+    ln_new, lm1_new, lm2_new, loss_o, mean_o, dh_o = refs[12:18]
+    scratch = refs[18:]
+    big_buf, small_buf, ln_res, loss_res, mean_res = scratch[:3], scratch[3:9], scratch[9:12], scratch[12], scratch[13]
+    in_sem, small_sem, out_sem, sout_sem = scratch[14:]
+    tiles = row_tiles(big_in[0].shape[0], COPY_TILE)
     small = [pltpu.make_async_copy(s, d, small_sem.at[i]) for i, (s, d) in enumerate(zip(small_in, small_buf))]
     reads = [[pltpu.make_async_copy(s.at[pl.ds(r0, n)], d.at[pl.ds(r0, n)], in_sem.at[t, i])
               for i, (s, d) in enumerate(zip(big_in, big_buf))] for t, (r0, n) in enumerate(tiles)]
@@ -445,17 +459,10 @@
     for row in reads[1:]:
         for cp in row:
             cp.start()
-    writes = []
     for t, (r0, n) in enumerate(tiles):
-        for cp in reads[t]:
-            cp.wait()
-        sl = slice(r0, r0 + n)
-        grad, emb, m1, m2 = [b[sl, :] for b in big_buf]
-        res = adam_step(emb.astype(F32), grad, m1, m2, WEIGHT_DECAY)
-        for i, (buf, dst, val) in enumerate(zip(big_res, (e_new, m1_new, m2_new), res)):
-            buf[sl, :] = val.astype(buf.dtype)
-            writes.append(pltpu.make_async_copy(buf.at[pl.ds(r0, n)], dst.at[pl.ds(r0, n)], out_sem.at[i]))
-            writes[-1].start()
+        for i, (buf, dst) in enumerate(zip(big_buf, big_out)):
+            reads[t][i].wait()
+            pltpu.make_async_copy(buf.at[pl.ds(r0, n)], dst.at[pl.ds(r0, n)], out_sem.at[i]).start()
     for cp in small:
         cp.wait()
     dln, lnp, lm1, lm2, sm, dh = small_buf
@@ -463,12 +470,13 @@
         buf[...] = val
     loss_res[...] = sm[0:1, :]
     mean_res[...] = sm[1:2, 0:1]
+    writes = []
     for i, (src, dst) in enumerate(zip((*ln_res, loss_res, mean_res, dh), (ln_new, lm1_new, lm2_new, loss_o, mean_o, dh_o))):
         writes.append(pltpu.make_async_copy(src, dst, sout_sem.at[i]))
         writes[-1].start()
-    for i, buf in enumerate(big_res):
-        pltpu.make_async_copy(buf, (e_new, m1_new, m2_new)[i], out_sem.at[i]).wait()
-    for cp in writes[-6:]:
+    for i, buf in enumerate(big_buf):
+        writes.append(pltpu.make_async_copy(buf, big_out[i], out_sem.at[i]))
+    for cp in writes:
         cp.wait()
 
 
@@ -492,11 +500,12 @@
         big = jax.ShapeDtypeStruct((voc, dim), F32)
         ln_s, sm_s = jax.ShapeDtypeStruct((2, dim), F32), jax.ShapeDtypeStruct((8, tok), F32)
         dh_s = jax.ShapeDtypeStruct((tok, dim), BF16)
-        dE, dh, dln, sm = pl.pallas_call(
+        big_b = jax.ShapeDtypeStruct((voc, dim), BF16)
+        e_new, m1n, m2n, dh, dln, sm = pl.pallas_call(
             functools.partial(step_kernel, side),
-            out_shape=[big, dh_s, ln_s, sm_s],
-            in_specs=[ANY] * 5,
-            out_specs=[ANY] * 4,
+            out_shape=[big_b, big, big, dh_s, ln_s, sm_s],
+            in_specs=[ANY] * 7,
+            out_specs=[ANY] * 6,
             scratch_shapes=[
                 vm((tok, dim), BF16), *[vm((1, tok), jnp.int32)] * 2, vm((2, dim), F32),
                 vm((tok, dim), BF16), vm((2, dim), F32), vm((8, tok), F32),
@@ -517,28 +526,28 @@
                 vm((2 * len(row_tiles(voc, TILE)), nck, ct), F32), *[vm((nck, ct), F32)] * 3,
                 vm((4, 8, tok), F32),
                 vm((ntp, 8, tok), F32),
-                dma((5,)), dma((4,)), dma(()), dma((2, 2, 2)), dma((2, 4, 2)), dma((2, 4)),
+                dma((5,)), dma((4,)), dma((3,)), dma(()), dma((2, 2, 2)), dma((2, 4, 2)), dma((2, 4)),
                 dma(()), dma(()), dma(()), dma((nck,)), dma(()), dma(()),
                 dma(()), dma((2, side, 3)), dma((2, 3)), dma(()), dma(()), *[dma((4,))] * 2,
                 pltpu.SemaphoreType.REGULAR,
             ],
             compiler_params=pltpu.CompilerParams(collective_id=0, has_side_effects=True, vmem_limit_bytes=67043328),
             name="head_step",
-        )(hidden, targets.reshape(1, tok), loss_mask.reshape(1, tok), ln_params, out_embed)
-
-        big_b, nt = jax.ShapeDtypeStruct((voc, dim), BF16), len(row_tiles(voc, 272))
-        shapes = [big, big_b, big, big, ln_s, ln_s, ln_s, ln_s, sm_s, dh_s]
-        outs = [big_b, big, big, ln_s, ln_s, ln_s, jax.ShapeDtypeStruct((1, tok), F32), jax.ShapeDtypeStruct((1, 1), F32), dh_s]
+        )(hidden, targets.reshape(1, tok), loss_mask.reshape(1, tok), ln_params, out_embed, embed_mom1, embed_mom2)
+
+        nt = len(row_tiles(voc, COPY_TILE))
+        bigs, smalls = [big_b, big, big], [ln_s, ln_s, ln_s, ln_s, sm_s, dh_s]
+        outs = [ln_s, ln_s, ln_s, jax.ShapeDtypeStruct((1, tok), F32), jax.ShapeDtypeStruct((1, 1), F32), dh_s]
         e_new, m1n, m2n, lnn, lm1n, lm2n, loss, mean, dh = pl.pallas_call(
-            adam_kernel,
-            out_shape=outs,
-            in_specs=[ANY] * len(shapes),
-            out_specs=[ANY] * len(outs),
-            scratch_shapes=[vm(s.shape, s.dtype) for s in shapes + outs[:8]]
-            + [dma((nt, 4)), dma((6,)), dma((3,)), dma((6,))],
+            finish_kernel,
+            out_shape=bigs + outs,
+            in_specs=[ANY] * 9,
+            out_specs=[ANY] * 9,
+            scratch_shapes=[vm(s.shape, s.dtype) for s in bigs + smalls + outs[:5]]
+            + [dma((nt, 3)), dma((6,)), dma((3,)), dma((6,))],
             compiler_params=pltpu.CompilerParams(vmem_limit_bytes=67043328),
-            name="adam_step",
-        )(dE, out_embed, embed_mom1, embed_mom2, dln, ln_params, ln_mom1, ln_mom2, sm, dh)
+            name="finish",
+        )(e_new, m1n, m2n, dln, ln_params, ln_mom1, ln_mom2, sm, dh)
         return (loss.reshape(tok), mean.reshape(1), dh, lnn, lm1n, lm2n, e_new, m1n, m2n)
 
     return jax.shard_map(device_step, mesh=mesh, in_specs=(row_spec, tok_spec, tok_spec, repl_spec, vocab_spec, repl_spec, repl_spec, vocab_spec, vocab_spec), out_specs=(tok_spec, P("dp"), row_spec, part_spec, part_spec, part_spec, row_spec, row_spec, row_spec), check_vma=False)

time: 76.3 us -> 74.4 us (0.975)
  Pallas kernels: 75.4 us -> 73.5 us
    pallas_call x2, Pallas kernels: 75.4 us -> 73.5 us  [the longest x1 67.1 us: device_step(): pl.pallas_call(functools.partial(step_kernel, side), out_shape=[big_b, bi...]
where the time goes in v4:
time: 74.4 us; the launch traced here: 74.3 us
  Pallas kernels  73.5 us (99%)
  between operations  0.83 us (1%)
    pallas_call x1, Pallas kernels, device_step(): pl.pallas_call(functools.partial(step_kernel, side), out_shape=[big_b, bi...  67.1 us
    pallas_call x1, Pallas kernels, device_step(): pl.pallas_call(finish_kernel, out_shape=bigs + outs, in_specs=[ANY] * 9,...  6.36 us

profile of v4, /device:TPU:97, one launch (start us, length us, event | category | flops | bytes accessed | tf_op | source)
XLA Modules:
  0.0 74.3 jit_solution(5084403094748063489)
XLA Ops:
  0.6 67.1 %head_step.1 = (bf16[1572,512]{1,0:T(8,128)(2,1)}, f32[1572,512]{1,0:T(8,128)}, f32[1572,512]{1,0:T(8,128)}, bf16[128,512]{1,0:T(8,128)(2,1)}, f32[2,512]{1,0:T(2,128)}, /*index=5*/f32[8,128]{1,0:T(8,128)}) custom-call(bf16[128,512]{1,0:T(8,128)(2,1)} %hid_hbm.1, s32[1,128]{1,0:T(1,128)} %bitcast.4, s32[1,128]{1,0:T(1,128)} %bitcast.5, f32[2,512]{1,0:T(2,128)} %refs_4_.1, ...), custom_call_target="tpu_custom_call" | custom-call | tf_op jit(solution)/shard_map/head_step/pallas_call | solution.py:504
  67.8 6.4 %finish.1 = (bf16[1572,512]{1,0:T(8,128)(2,1)}, f32[1572,512]{1,0:T(8,128)}, f32[1572,512]{1,0:T(8,128)}, f32[2,512]{1,0:T(2,128)}, f32[2,512]{1,0:T(2,128)}, /*...) custom-call(bf16[1572,512]{1,0:T(8,128)(2,1)} %get-tuple-element.24.refs_0_, ...), custom_call_target="tpu_custom_call" | custom-call | tf_op jit(solution)/shard_map/finish/pallas_call | solution.py:541

commit v5 on v4

--- a/solution.py
+++ b/solution.py
@@ -336,8 +336,8 @@
                 ring1(1, dy, k).start()
         direct1(1, dy, 1 - odd if dj else odd)
 
+    grad_step(2, 1)
     grad_step(2, 0)
-    grad_step(2, 1)
     grad_step(plus, 1)
     grad_step(minus, 1)
     grad_step(0, 1)

time: 74.4 us -> 73.3 us (0.985)
  Pallas kernels: 73.5 us -> 72.3 us
    pallas_call x1, Pallas kernels: 67.1 us -> 66 us  [device_step(): pl.pallas_call(functools.partial(step_kernel, side), out_shape=[big_b, bi...]
where the time goes in v5:
time: 73.3 us; the launch traced here: 73.2 us
  Pallas kernels  72.3 us (99%)
  between operations  0.83 us (1%)
    pallas_call x1, Pallas kernels, device_step(): pl.pallas_call(functools.partial(step_kernel, side), out_shape=[big_b, bi...  66 us
    pallas_call x1, Pallas kernels, device_step(): pl.pallas_call(finish_kernel, out_shape=bigs + outs, in_specs=[ANY] * 9,...  6.36 us

profile of v5, /device:TPU:97, one launch (start us, length us, event | category | flops | bytes accessed | tf_op | source)
XLA Modules:
  0.0 73.2 jit_solution(7907149550591878860)
XLA Ops:
  0.6 66.0 %head_step.1 = (bf16[1572,512]{1,0:T(8,128)(2,1)}, f32[1572,512]{1,0:T(8,128)}, f32[1572,512]{1,0:T(8,128)}, bf16[128,512]{1,0:T(8,128)(2,1)}, f32[2,512]{1,0:T(2,128)}, /*index=5*/f32[8,128]{1,0:T(8,128)}) custom-call(bf16[128,512]{1,0:T(8,128)(2,1)} %hid_hbm.1, s32[1,128]{1,0:T(1,128)} %bitcast.4, s32[1,128]{1,0:T(1,128)} %bitcast.5, f32[2,512]{1,0:T(2,128)} %refs_4_.1, ...), custom_call_target="tpu_custom_call" | custom-call | tf_op jit(solution)/shard_map/head_step/pallas_call | solution.py:504
  66.6 6.4 %finish.1 = (bf16[1572,512]{1,0:T(8,128)(2,1)}, f32[1572,512]{1,0:T(8,128)}, f32[1572,512]{1,0:T(8,128)}, f32[2,512]{1,0:T(2,128)}, f32[2,512]{1,0:T(2,128)}, /*...) custom-call(bf16[1572,512]{1,0:T(8,128)(2,1)} %get-tuple-element.24.refs_0_, ...), custom_call_target="tpu_custom_call" | custom-call | tf_op jit(solution)/shard_map/finish/pallas_call | solution.py:541
